TPU v7x, 128 devices: a whole 4x4x4 slice. The times are simulated.
128 devices in a mesh: ep: 32 (over x, z, core), etp: 4 (over y).
Axes of the slice: x: 4, y: 4, z: 4, core: 2. Of those that a mesh axis runs over, the one named last changes fastest.
Arguments:
- tokens: bfloat16 [4096, 4096], P('ep', 'etp'), may hold values from -6 to 6
- expert_ids: int32 [4096, 8], P('ep'), may hold values from 0 to 63, all different within a row; in each aligned block of 128 rows (0 to 127, 128 to 255, ...) at most 24 rows name the same one
- gate_prob: float32 [4096, 8], P('ep'), may hold values from 0.05 to 1
- gate_weight: bfloat16 [64, 4096, 1536], P('ep', None, 'etp'), may hold values from -0.09375 to 0.09375
- up_weight: bfloat16 [64, 4096, 1536], P('ep', None, 'etp'), may hold values from -0.09375 to 0.09375
- down_weight: bfloat16 [64, 1536, 4096], P('ep', 'etp'), may hold values from -0.15625 to 0.15625
Outputs:
- mixed: bfloat16 [4096, 4096], P('ep', 'etp')
Inputs may be any that keep to these rules, and one draw needn't show every extreme that they name: `expert_ids`: each row names 8 different experts. Within each aligned block of 128 rows (one token group) no expert is named more than 24 times, and in every draw some expert is named exactly 24 times in some block.
All inputs are finite; a program needn't handle non-finite values.
Results may differ from a plain program's by a relative error of at most 0.012.
Values may be sent and summed in bfloat16 or wider, within the bound.
No kernel may reach another device: no remote copies, remote signals or barrier semaphores. Data moves between devices by JAX's collectives and lax.ppermute only.
A program may use at most 128 MiB of HBM per device.

v0:
```python
import jax
import jax.numpy as jnp
from jax import lax
from jax.experimental import pallas as pl
from jax.experimental.pallas import tpu as pltpu
from jax.sharding import PartitionSpec as P


SIDE = 4
CAP = 24
TOK = 128
F = 512
K = SIDE * F
FF = 384
BF = jnp.bfloat16
F32 = jnp.float32
VMEM = 60 * 1024 * 1024
PIECES = [(s, dc) for dc in range(2) for s in range(SIDE)]


def ep_of(x, z, c):
    return ((x % SIDE) * SIDE + z % SIDE) * 2 + c


def recv(a, dim, d, flip=0):
    if dim == "y":
        return lax.ppermute(a, "etp", [((i + d) % SIDE, i) for i in range(SIDE)])
    dx, dz = (d, 0) if dim == "x" else (0, d)
    pairs = [(ep_of(x + dx, z + dz, c ^ flip), ep_of(x, z, c))
             for x in range(SIDE) for z in range(SIDE) for c in range(2)]
    return lax.ppermute(a, "ep", pairs)


def dot(a, b):
    return jnp.dot(a, b, preferred_element_type=F32)


def call(kernel, grid, in_specs, out_specs, out_shapes, scratch=()):
    return pl.pallas_call(
        kernel, grid=grid, in_specs=in_specs, out_specs=out_specs, out_shape=[jax.ShapeDtypeStruct(s, BF) for s in out_shapes],
        scratch_shapes=scratch,
        compiler_params=pltpu.CompilerParams(vmem_limit_bytes=VMEM, dimension_semantics=("arbitrary",) * len(grid)))


PAIRS = pl.BlockSpec((2, 256, 768), lambda i: (0, 0, 0))
COLS = 512
META = pl.BlockSpec((16, TOK), lambda i: (0, K // TOK))
DENSE = pl.BlockSpec((TOK, COLS), lambda i: (0, i))
PART = pl.BlockSpec((TOK // 2, COLS), lambda i: (0, i))
ROWS = pl.BlockSpec((2, 96, COLS), lambda i: (0, 0, i))
NEAR = [DENSE, DENSE, PART, PART, DENSE]


def select_body(where, *refs):
    xs, metas, outs, (p,) = refs[:10], refs[10:18], refs[18:34], refs[34:]

    @pl.when(pl.program_id(0) == 0)
    def _():
        shape = (TOK, TOK)
        before = jnp.where(lax.broadcasted_iota(jnp.int32, shape, 0) < lax.broadcasted_iota(jnp.int32, shape, 1), 1.0, 0.0).astype(BF)
        slot = lax.broadcasted_iota(jnp.int32, (CAP, TOK), 0).astype(F32)
        q = lax.broadcasted_iota(jnp.int32, (16, TOK), 0)
        step, flip = (q // 2) % SIDE, q // 8
        x, z, c = where[0], where[1], where[2]
        core = jnp.where(flip == 1, 1 - c, c)
        for h in range(2):
            zz = (z + step) % SIDE if h == 0 else z
            xx = x if h == 0 else (x + step) % SIDE
            names = (((xx * SIDE + zz) * 2 + core) * 2 + q % 2).astype(F32)
            for g in range(4):
                ids = metas[h * 4 + g][...].astype(F32)
                match = jnp.zeros((16, TOK), F32)
                for k in range(8):
                    match = match + jnp.where(ids[k:k + 1] == names, 1.0, 0.0)
                place = jnp.where(match > 0.0, dot(match.astype(BF), before), -1.0)
                for n in range(0, 16, 2):
                    two = jnp.concatenate([jnp.where(place[n + e:n + e + 1] == slot, 1.0, 0.0) for e in range(2)], axis=0)
                    p[h * 4 + g, n * CAP:n * CAP + 48, :] = two.astype(BF)

    for h in range(2):
        x0, x1, x2a, x2b, x3 = [r[...] for r in xs[h * 5:h * 5 + 5]]
        dense = [x0, x1, jnp.concatenate([x2a, x2b], axis=0), x3]
        for part in range(2):
            rows = [dot(p[h * 4 + g, part * 192:part * 192 + 192, :], dense[g]) for g in range(4)]
            for n in range(4):
                for e in range(2):
                    at = n * 48 + e * CAP
                    outs[h * 8 + part * 4 + n][e] = jnp.concatenate([r[at:at + CAP] for r in rows], axis=0).astype(BF)


def select(where, near):
    metas = [b for n in near for b in (n[0], n[1], n[2], n[4])]
    return call(select_body, (K // COLS,), [pl.BlockSpec(memory_space=pltpu.SMEM)] + NEAR * 2 + [META] * 8, [ROWS] * 16, [(2, 96, K)] * 16,
                [pltpu.VMEM((8, 384, TOK), BF)])(where, *near[0], *near[1], *metas)


def combine_body(*refs):
    tables, rows, outs = refs[:2], refs[2:18], refs[18:]
    for h in range(2):
        o = outs[h * 7:h * 7 + 7]
        for k in range(2):
            picked = jnp.concatenate([r[e, k * 48:k * 48 + 48, :] for r in rows[h * 8:h * 8 + 8] for e in range(2)], axis=0)
            dense = dot(tables[h][k], picked).astype(BF)
            quarters = [dense[n * 64:n * 64 + 64] for n in range(4)]
            if k == 0:
                o[0][...] = dense[:TOK]
                quarters = quarters[2:]
            for n, part in enumerate(quarters):
                o[(1 if k == 0 else 3) + n][...] = part


def combine(tables, rows):
    shapes = [(TOK, K)] + [(TOK // 2, K)] * 6
    return call(combine_body, (K // COLS,), [PAIRS] * 2 + [ROWS] * 16, ([DENSE] + [PART] * 6) * 2, shapes * 2)(*tables, *rows[0], *rows[1])


def experts_body(y_ref, *refs):
    pieces, (wg, wu, wd), outs = refs[:8], refs[8:11], refs[11:19]
    gate, up, down, lhs, acc, hs, hid, res, sems, out_sems = refs[19:]
    e = pl.program_id(0)
    y = y_ref[0]

    def stage(k, n):
        if n == 2:
            return [pltpu.make_async_copy(wd.at[k], down.at[k], sems.at[k, 24])]
        copies = []
        for s in range(SIDE):
            copies.append(pltpu.make_async_copy(pieces[n * SIDE + s].at[k], lhs.at[k, n, pl.ds(s * 96, 96), :], sems.at[k, n * 12 + s]))
        for dy in range(SIDE):
            src = pl.ds(pl.multiple_of(lax.rem(y + dy, SIDE) * 1024 + n * F, 128), F)
            dst = pl.ds(n * K + dy * F, F)
            copies.append(pltpu.make_async_copy(wg.at[k, src, :], gate.at[k, dst, :], sems.at[k, n * 12 + 4 + dy]))
            copies.append(pltpu.make_async_copy(wu.at[k, src, :], up.at[k, dst, :], sems.at[k, n * 12 + 8 + dy]))
        return copies

    def start(k, n):
        for cp in stage(k, n):
            cp.start()

    def wait(n):
        for cp in stage(e, n):
            cp.wait()

    def results(k, half):
        return [pltpu.make_async_copy(res.at[k, half, pl.ds(s * 96, 96), :], outs[half * SIDE + s].at[k], out_sems.at[k, half * SIDE + s])
                for s in range(SIDE)]

    @pl.when(e == 0)
    def _():
        for k in range(2):
            for n in range(3):
                start(k, n)

    @pl.loop(0, 2)
    def _(half):
        for n in range(2):
            @pl.when(half == n)
            def _(n=n):
                wait(n)
        rows = pl.ds(pl.multiple_of(half * K, K), K)
        for n, w in enumerate((gate, up)):
            acc[half, :, n * FF:(n + 1) * FF] = dot(lhs[e, half], w[e, rows, :])

    @pl.loop(0, SIDE * SIDE)
    def _(n):
        to = pl.ds(pl.multiple_of(n * CAP, 8), CAP)
        fro = pl.ds(pl.multiple_of(((n % SIDE) * SIDE + n // SIDE) * CAP, 8), CAP)
        v = acc[1, to, :] + acc[0, fro, :]
        g, u = v[:, :FF], v[:, FF:]
        hs[to, :] = g * (1.0 / (1.0 + jnp.exp(-g))) * u

    hid[0] = jnp.concatenate([hs[(j * SIDE + i) * CAP:(j * SIDE + i + 1) * CAP, :] for i in range(SIDE) for j in range(SIDE)], axis=0).astype(BF)
    hid[1] = hs[...].astype(BF)
    wait(2)

    @pl.loop(0, 2 * SIDE)
    def _(n):
        half, dy = n // SIDE, n % SIDE
        src = pl.ds(pl.multiple_of(lax.rem(y + dy, SIDE) * 1024 + half * F, F), F)
        res[e, half, :, pl.ds(pl.multiple_of(dy * F, F), F)] = dot(hid[half], down[e, :, src]).astype(BF)
        for k in range(2):
            @pl.when(n == k * SIDE + SIDE - 1)
            def _(k=k):
                for cp in results(e, k):
                    cp.start()

    @pl.when(e == 1)
    def _():
        for k in range(2):
            for half in range(2):
                for cp in results(k, half):
                    cp.wait()


def experts(y, a, b, wg, wu, wd):
    hbm = pl.BlockSpec(memory_space=pl.ANY)
    scratch = [pltpu.VMEM((2, 2 * K, FF), BF), pltpu.VMEM((2, 2 * K, FF), BF), pltpu.VMEM((2, FF, 2 * K), BF), pltpu.VMEM((2, 2, 384, K), BF),
               pltpu.VMEM((2, 384, 2 * FF), F32), pltpu.VMEM((384, FF), F32), pltpu.VMEM((2, 384, FF), BF), pltpu.VMEM((2, 2, 384, K), BF),
               pltpu.SemaphoreType.DMA((2, 25)), pltpu.SemaphoreType.DMA((2, 8))]
    o = call(experts_body, (2,), [pl.BlockSpec(memory_space=pltpu.SMEM)] + [hbm] * 11, [hbm] * 8,
             [(2, 96, K)] * 8, scratch)(y, *a, *b, wg, wu, wd)
    return o[:4], o[4:]


def weighted_table(info, names):
    columns = jnp.stack(info).astype(F32)
    ids, prob = columns[:, :8], columns[:, 8:]
    hit = ids[:, None, :, :] == names[None, :, None, None]
    match = jnp.any(hit, axis=2)
    weight = jnp.sum(jnp.where(hit, prob[:, None, :, :], 0.0), axis=2)
    t = jnp.arange(TOK)
    before = (t[:, None] < t[None, :]).astype(BF)
    place = jnp.einsum("get,tu->geu", match.astype(BF), before, preferred_element_type=F32)
    place = jnp.where(match, place, -1.0).reshape(2, 2, 16, TOK).transpose(0, 2, 1, 3)
    weight = weight.reshape(2, 2, 16, TOK).transpose(0, 2, 1, 3)
    eye = jnp.arange(2)
    same = (eye[:, None] == eye[None, :])[None, None, :, None, :, None]
    on = (place[:, :, None, None, :, :] == jnp.arange(CAP, dtype=F32)[None, None, None, :, None, None]) & same
    wgt = jnp.where(on, weight[:, :, None, None, :, :], 0.0).astype(BF)
    return wgt.reshape(2, 768, 256).swapaxes(1, 2)


def total(terms):
    out = terms[0].astype(F32)
    for t in terms[1:]:
        out = out + t.astype(F32)
    return out


def gather_ring(a, dim):
    half = a.shape[0] // 2
    r1, r3 = recv(a, dim, 1), recv(a, dim, -1)
    return [a, r1, recv(r1[:half], dim, 1), recv(r3[half:], dim, -1), r3]


def scatter_ring(blocks, dim):
    b0, b10, b11, b20, b21, b30, b31 = blocks
    s0, s1 = recv(b20, dim, -1), recv(b21, dim, 1)
    i1, j0 = recv(b11, dim, -1), recv(b30, dim, 1)
    i0 = recv(total([b10, s0]).astype(BF), dim, -1)
    j1 = recv(total([b31, s1]).astype(BF), dim, 1)
    half = b20.shape[0]
    return jnp.concatenate([total([b0[:half], i0, j0]), total([b0[half:], i1, j1])], axis=0)


def body(tokens, expert_ids, gate_prob, gate_weight, up_weight, down_weight):
    ep = lax.axis_index("ep")
    x, z, c = ep // 8, (ep // 2) % SIDE, ep % 2
    where = jnp.stack([x, z, c]).astype(jnp.int32)
    y = lax.axis_index("etp").astype(jnp.int32).reshape(1)
    meta = jnp.concatenate([expert_ids.T.astype(BF), gate_prob.T.astype(BF), jnp.zeros((112, TOK), BF)], axis=0)
    wide = [tokens] + [recv(tokens, "y", d) for d in (1, 2, 3)]
    axes = (("x", "z"), ("z", "x"))
    near = [gather_ring(jnp.concatenate([w[:, h * F:(h + 1) * F] for w in wide] + [meta], axis=1), dim)
            for h, (dim, far) in enumerate(axes)]
    picked = select(where, near)
    rows, got, tables = [{}, {}], [{}, {}], []
    for h, (dim, far) in enumerate(axes):
        mates = []
        for s, dc in PIECES:
            mate = ep_of(x, z + s, c ^ dc) if far == "z" else ep_of(x + s, z, c ^ dc)
            mates += [2 * mate, 2 * mate + 1]
            out = picked[h * 8 + PIECES.index(((-s) % SIDE, dc))]
            rows[h][s, dc] = out if (s, dc) == (0, 0) else recv(out, far, s, dc)
        n = near[h]
        tables.append(weighted_table([m[:16, K:] for m in (n[0], n[1], n[2], n[4])], jnp.stack(mates).astype(F32)))
    for dc in range(2):
        outs = experts(y, *[[rows[h][s, dc] for s in range(SIDE)] for h in range(2)], gate_weight, up_weight, down_weight)
        for h, (dim, far) in enumerate(axes):
            for s in range(SIDE):
                out = outs[h][(-s) % SIDE]
                got[h][s, dc] = out if (s, dc) == (0, 0) else recv(out, far, s, dc)
    dense = combine(tables, [[got[h][q] for q in PIECES] for h in range(2)])
    halves = [scatter_ring(dense[h * 7:h * 7 + 7], dim).astype(BF) for h, (dim, far) in enumerate(axes)]
    parts = [jnp.concatenate([halves[h][:, d * F:(d + 1) * F] for h in range(2)], axis=1) for d in range(SIDE)]
    return total([parts[0]] + [recv(parts[d], "y", -d) for d in (1, 2, 3)]).astype(BF)


def solution(mesh):
    in_specs = (P("ep", "etp"), P("ep", None), P("ep", None), P("ep", None, "etp"), P("ep", None, "etp"), P("ep", "etp", None))

    return jax.shard_map(body, mesh=mesh, in_specs=in_specs, out_specs=P("ep", "etp"), check_vma=False)
```

profile of v0, /device:TPU:1, one launch (start us, length us, event | category | flops | bytes accessed | tf_op | source)
XLA Modules:
  0.0 319.5 jit_solution(13601675396410310394)
XLA Ops:
  0.0 3.6 %collective-permute-start = (bf16[128,1024]{1,0:T(8,128)(2,1)}, bf16[128,1024]{1,0:T(8,128)(2,1)S(1)}, u32[]{:S(2)}, u32[]{:S(2)}) collective-permute-start(bf16[128,1024]{1,0:T(8,128)(2,1)} %param.6), channel_id=1, source_target_pairs={{1,0},{2,1},{3,2},{0,3},{5,4},{6,5},{7,6},{4,7},{9,8},{10,9},{11,1... | collective-permute-start | bytes 786440 | tf_op jit(solution)/shard_map/ppermute | solution.py:27
  4.6 1.0 slice_dynamic-update-slice_fusion.6
  7.1 7.3 %collective-permute-done = bf16[128,1024]{1,0:T(8,128)(2,1)S(1)} collective-permute-done((bf16[128,1024]{1,0:T(8,128)(2,1)}, bf16[128,1024]{1,0:T(8,128)(2,1)S(1)}, u32[]{:S(2)}, u32[]{:S(2)}) %collective-permute-start) | collective-permute-done | bytes 262176 | tf_op jit(solution)/shard_map/ppermute | solution.py:27
  14.4 4.7 %collective-permute-done.2 = bf16[128,1024]{1,0:T(8,128)(2,1)S(1)} collective-permute-done((bf16[128,1024]{1,0:T(8,128)(2,1)}, bf16[128,1024]{1,0:T(8,128)(2,1)S(1)}, u32[]{:S(2)}, u32[]{:S(2)}) %collective-permute-start.2) | collective-permute-done | bytes 262176 | tf_op jit(solution)/shard_map/ppermute | solution.py:27
  19.3 1.7 collective-permute-start.8
  21.0 2.2 collective-permute-start.6
  23.2 1.2 collective-permute-start.5
  24.4 1.5 collective-permute-start.3
  25.8 9.8 %collective-permute-done.8.refs_9_.refs_17_ = bf16[128,2176]{1,0:T(8,128)(2,1)S(1)} collective-permute-done((bf16[128,2176]{1,0:T(8,128)(2,1)S(1)}, bf16[128,2176]{1,0:T(8,128)(2,1)S(1)}, u32[]{:S(2)}, u32[]{:S(2)}) %collective-permute-start.8) | collective-permute-done | bytes 557088 | tf_op jit(solution)/shard_map/ppermute | solution.py:31
  37.2 2.7 collective-permute-start.7
  40.7 1.2 collective-permute-start.9
  42.7 1.5 collective-permute-start.4
  45.0 3.8 %collective-permute-done.9.refs_3_ = bf16[64,2176]{1,0:T(8,128)(2,1)} collective-permute-done((bf16[64,2176]{1,0:T(8,128)(2,1)}, bf16[64,2176]{1,0:T(8,128)(2,1)}, u32[]{:S(2)}, u32[]{:S(2)}) %collective-permute-start.9) | collective-permute-done | bytes 278560 | tf_op jit(solution)/shard_map/ppermute | solution.py:31
  49.3 8.6 %shard_map.64 = (bf16[2,96,2048]{2,1,0:T(8,128)(2,1)}, bf16[2,96,2048]{2,1,0:T(8,128)(2,1)}, bf16[2,96,2048]{2,1,0:T(8,128)(2,1)}, bf16[2,96,2048]{2,1,0:T(8,128...) custom-call(s32[3]{0:T(128)} %pad_add_fusion.where, ...), custom_call_target="tpu_custom_call" | custom-call | tf_op jit(solution)/shard_map/pallas_call | solution.py:93
  59.5 2.7 collective-permute-start.14
  62.5 12.2 %collective-permute-done.11.refs_1_ = bf16[2,96,2048]{2,1,0:T(8,128)(2,1)S(1)} collective-permute-done((bf16[2,96,2048]{2,1,0:T(8,128)(2,1)}, bf16[2,96,2048]{2,1,0:T(8,128)(2,1)S(1)}, u32[]{:S(2)}, u32[]{:S(2)}) %collective-permute-start.11) | collective-permute-done | bytes 786464 | tf_op jit(solution)/shard_map/ppermute | solution.py:31
  74.7 1.2 collective-permute-start.16
  76.2 7.1 %collective-permute-start.20 = (bf16[2,96,2048]{2,1,0:T(8,128)(2,1)}, bf16[2,96,2048]{2,1,0:T(8,128)(2,1)S(1)}, u32[]{:S(2)}, u32[]{:S(2)}) collective-permute-start(bf16[2,96,2048]{2,1,0:T(8,128)(2,1)} %get-tuple-element.63), channel_id=1, source_target_pairs={{4,0},{0,4},{12,8},{8,12},{20,16},{16,20},{28,24},{24,28},{36,32},... | collective-permute-start | bytes 2359304 | tf_op jit(solution)/shard_map/ppermute | solution.py:31
  83.2 13.0 %collective-permute-done.13.refs_3_ = bf16[2,96,2048]{2,1,0:T(8,128)(2,1)S(1)} collective-permute-done((bf16[2,96,2048]{2,1,0:T(8,128)(2,1)}, bf16[2,96,2048]{2,1,0:T(8,128)(2,1)S(1)}, u32[]{:S(2)}, u32[]{:S(2)}) %collective-permute-start.13) | collective-permute-done | bytes 786464 | tf_op jit(solution)/shard_map/ppermute | solution.py:31
  96.3 0.9 copy-done.10
  97.2 1.1 collective-permute-start.21
  99.3 1.3 collective-permute-start.22
  100.8 3.7 %collective-permute-start.25 = (bf16[2,96,2048]{2,1,0:T(8,128)(2,1)}, bf16[2,96,2048]{2,1,0:T(8,128)(2,1)}, u32[]{:S(2)}, u32[]{:S(2)}) collective-permute-start(bf16[2,96,2048]{2,1,0:T(8,128)(2,1)} %get-tuple-element.68), channel_id=1, source_target_pairs={{36,0},{32,4},{44,8},{40,12},{52,16},{48,20},{60,24},{56,28},{68,3... | collective-permute-start | bytes 2359304 | tf_op jit(solution)/shard_map/ppermute | solution.py:31
  104.5 13.2 %collective-permute-done.21.refs_1_ = bf16[2,96,2048]{2,1,0:T(8,128)(2,1)S(1)} collective-permute-done((bf16[2,96,2048]{2,1,0:T(8,128)(2,1)}, bf16[2,96,2048]{2,1,0:T(8,128)(2,1)S(1)}, u32[]{:S(2)}, u32[]{:S(2)}) %collective-permute-start.21) | collective-permute-done | bytes 786464 | tf_op jit(solution)/shard_map/ppermute | solution.py:31
  117.6 2.1 collective-permute-start.26
  122.5 18.5 %shard_map.65 = (bf16[2,96,2048]{2,1,0:T(8,128)(2,1)}, bf16[2,96,2048]{2,1,0:T(8,128)(2,1)}, bf16[2,96,2048]{2,1,0:T(8,128)(2,1)}, bf16[2,96,2048]{2,1,0:T(8,128...) custom-call(s32[1]{0:T(128)} %bitcast.48.y_ref, ...), custom_call_target="tpu_custom_call" | custom-call | tf_op jit(solution)/shard_map/pallas_call | solution.py:200
  141.0 1.5 collective-permute-start.27
  142.5 1.8 collective-permute-start.17
  144.9 1.8 collective-permute-start.32
  148.3 14.2 %collective-permute-done.27.refs_7_ = bf16[2,96,2048]{2,1,0:T(8,128)(2,1)S(1)} collective-permute-done((bf16[2,96,2048]{2,1,0:T(8,128)(2,1)}, bf16[2,96,2048]{2,1,0:T(8,128)(2,1)S(1)}, u32[]{:S(2)}, u32[]{:S(2)}) %collective-permute-start.27) | collective-permute-done | bytes 786464 | tf_op jit(solution)/shard_map/ppermute | solution.py:31
  162.6 0.9 copy-done.11
  163.5 18.5 %shard_map.66 = (bf16[2,96,2048]{2,1,0:T(8,128)(2,1)}, bf16[2,96,2048]{2,1,0:T(8,128)(2,1)}, bf16[2,96,2048]{2,1,0:T(8,128)(2,1)}, bf16[2,96,2048]{2,1,0:T(8,128...) custom-call(s32[1]{0:T(128)} %bitcast.48.y_ref, ...), custom_call_target="tpu_custom_call" | custom-call | tf_op jit(solution)/shard_map/pallas_call | solution.py:200
  182.6 1.5 collective-permute-start.29
  185.0 0.9 collective-permute-start.31
  185.9 16.5 %collective-permute-done.34.refs_13_ = bf16[2,96,2048]{2,1,0:T(8,128)(2,1)S(1)} collective-permute-done((bf16[2,96,2048]{2,1,0:T(8,128)(2,1)}, bf16[2,96,2048]{2,1,0:T(8,128)(2,1)S(1)}, u32[]{:S(2)}, u32[]{:S(2)}) %collective-permute-start.34) | collective-permute-done | bytes 786464 | tf_op jit(solution)/shard_map/ppermute | solution.py:31
  202.4 1.1 collective-permute-start.35
  203.5 18.3 %collective-permute-start.37 = (bf16[2,96,2048]{2,1,0:T(8,128)(2,1)}, bf16[2,96,2048]{2,1,0:T(8,128)(2,1)}, u32[]{:S(2)}, u32[]{:S(2)}) collective-permute-start(bf16[2,96,2048]{2,1,0:T(8,128)(2,1)} %get-tuple-element.81), channel_id=1, source_target_pairs={{68,0},{64,4},{76,8},{72,12},{84,16},{80,20},{92,24},{88,28},{100,... | collective-permute-start | bytes 2359304 | tf_op jit(solution)/shard_map/ppermute | solution.py:31
  221.9 0.9 copy-done.18
  223.8 1.1 and.126
  226.5 1.1 and.135
  230.6 1.8 fusion.1
  232.4 7.9 %collective-permute-done.37.refs_16_ = bf16[2,96,2048]{2,1,0:T(8,128)(2,1)} collective-permute-done((bf16[2,96,2048]{2,1,0:T(8,128)(2,1)}, bf16[2,96,2048]{2,1,0:T(8,128)(2,1)}, u32[]{:S(2)}, u32[]{:S(2)}) %collective-permute-start.37) | collective-permute-done | bytes 786464 | tf_op jit(solution)/shard_map/ppermute | solution.py:31
  240.3 16.7 %collective-permute-done.38.refs_17_ = bf16[2,96,2048]{2,1,0:T(8,128)(2,1)} collective-permute-done((bf16[2,96,2048]{2,1,0:T(8,128)(2,1)}, bf16[2,96,2048]{2,1,0:T(8,128)(2,1)}, u32[]{:S(2)}, u32[]{:S(2)}) %collective-permute-start.38) | collective-permute-done | bytes 786464 | tf_op jit(solution)/shard_map/ppermute | solution.py:31
  257.1 8.8 %shard_map.67 = (bf16[128,2048]{1,0:T(8,128)(2,1)}, bf16[64,2048]{1,0:T(8,128)(2,1)}, bf16[64,2048]{1,0:T(8,128)(2,1)}, bf16[64,2048]{1,0:T(8,128)(2,1)}, bf16[6...) custom-call(bf16[2,256,768]{2,1,0:T(8,128)(2,1)} %get-tuple-element., ...), custom_call_target="tpu_custom_call" | custom-call | tf_op jit(solution)/shard_map/pallas_call | solution.py:114
  265.9 2.7 collective-permute-start.41
  268.6 2.7 collective-permute-start.43
  271.3 3.5 %collective-permute-done.39 = bf16[64,2048]{1,0:T(8,128)(2,1)S(1)} collective-permute-done((bf16[64,2048]{1,0:T(8,128)(2,1)}, bf16[64,2048]{1,0:T(8,128)(2,1)S(1)}, u32[]{:S(2)}, u32[]{:S(2)}) %collective-permute-start.39) | collective-permute-done | bytes 262176 | tf_op jit(solution)/shard_map/ppermute | solution.py:31
  274.8 2.6 collective-permute-start.47
  277.4 1.0 add_convert_fusion.8
  278.4 1.1 collective-permute-done.43
  279.5 2.6 collective-permute-start.49
  282.1 1.0 add_convert_fusion.6
  283.2 1.0 add_convert_fusion.4
  284.2 4.0 %collective-permute-done.49 = bf16[64,2048]{1,0:T(8,128)(2,1)S(1)} collective-permute-done((bf16[64,2048]{1,0:T(8,128)(2,1)}, bf16[64,2048]{1,0:T(8,128)(2,1)S(1)}, u32[]{:S(2)}, u32[]{:S(2)}) %collective-permute-start.49) | collective-permute-done | bytes 262176 | tf_op jit(solution)/shard_map/ppermute | solution.py:31
  288.3 1.5 collective-permute-start.44
  289.8 1.0 add_convert_fusion.2
  290.9 1.8 collective-permute-start.46
  292.6 2.0 collective-permute-start.50
  294.6 1.3 add_convert_fusion.7
  295.9 2.2 collective-permute-done.48
  298.1 5.8 %collective-permute-done.46 = bf16[64,2048]{1,0:T(8,128)(2,1)S(1)} collective-permute-done((bf16[64,2048]{1,0:T(8,128)(2,1)S(1)}, bf16[64,2048]{1,0:T(8,128)(2,1)S(1)}, u32[]{:S(2)}, u32[]{:S(2)}) %collective-permute-start.46) | collective-permute-done | bytes 262176 | tf_op jit(solution)/shard_map/ppermute | solution.py:31
  304.8 2.7 collective-permute-start.53
  307.5 3.7 %collective-permute-done.52 = bf16[128,1024]{1,0:T(8,128)(2,1)S(1)} collective-permute-done((bf16[128,1024]{1,0:T(8,128)(2,1)S(1)}, bf16[128,1024]{1,0:T(8,128)(2,1)S(1)}, u32[]{:S(2)}, u32[]{:S(2)}) %collective-permute-start.52) | collective-permute-done | bytes 262176 | tf_op jit(solution)/shard_map/ppermute | solution.py:27
  311.2 7.4 %collective-permute-done.51 = bf16[128,1024]{1,0:T(8,128)(2,1)S(1)} collective-permute-done((bf16[128,1024]{1,0:T(8,128)(2,1)S(1)}, bf16[128,1024]{1,0:T(8,128)(2,1)S(1)}, u32[]{:S(2)}, u32[]{:S(2)}) %collective-permute-start.51) | collective-permute-done | bytes 262176 | tf_op jit(solution)/shard_map/ppermute | solution.py:27
  (156 shorter events, 24.5 us)
Async XLA Ops:
  0.0 14.3 %collective-permute-start = (bf16[128,1024]{1,0:T(8,128)(2,1)}, bf16[128,1024]{1,0:T(8,128)(2,1)S(1)}, u32[]{:S(2)}, u32[]{:S(2)}) collective-permute-start(bf16[128,1024]{1,0:T(8,128)(2,1)} %param.6), channel_id=1, source_target_pairs={{1,0},{2,1},{3,2},{0,3},{5,4},{6,5},{7,6},{4,7},{9,8},{10,9},{11,1... | collective-permute-start | bytes 786440 | tf_op jit(solution)/shard_map/ppermute | solution.py:27
  3.6 10.8 %collective-permute-start.1 = (bf16[128,1024]{1,0:T(8,128)(2,1)}, bf16[128,1024]{1,0:T(8,128)(2,1)S(1)}, u32[]{:S(2)}, u32[]{:S(2)}) collective-permute-start(bf16[128,1024]{1,0:T(8,128)(2,1)} %param.6), channel_id=1, source_target_pairs={{2,0},{3,1},{0,2},{1,3},{6,4},{7,5},{4,6},{5,7},{10,8},{11,9},{8,1... | collective-permute-start | bytes 786440 | tf_op jit(solution)/shard_map/ppermute | solution.py:27
  3.9 15.2 %collective-permute-start.2 = (bf16[128,1024]{1,0:T(8,128)(2,1)}, bf16[128,1024]{1,0:T(8,128)(2,1)S(1)}, u32[]{:S(2)}, u32[]{:S(2)}) collective-permute-start(bf16[128,1024]{1,0:T(8,128)(2,1)} %param.6), channel_id=1, source_target_pairs={{3,0},{0,1},{1,2},{2,3},{7,4},{4,5},{5,6},{6,7},{11,8},{8,9},{9,10... | collective-permute-start | bytes 786440 | tf_op jit(solution)/shard_map/ppermute | solution.py:27
  19.2 30.1 %copy-start.4 = (bf16[128,2176]{1,0:T(8,128)(2,1)}, bf16[128,2176]{1,0:T(8,128)(2,1)S(1)}, u32[]{:S(2)}) copy-start(bf16[128,2176]{1,0:T(8,128)(2,1)S(1)} %get-tuple-element.121.refs_5_.refs_14_) | copy-start | bytes 1671172
  19.2 30.1 %copy-start.5 = (bf16[128,2176]{1,0:T(8,128)(2,1)}, bf16[128,2176]{1,0:T(8,128)(2,1)S(1)}, u32[]{:S(2)}) copy-start(bf16[128,2176]{1,0:T(8,128)(2,1)S(1)} %get-tuple-element.122.refs_0_.refs_10_) | copy-start | bytes 1671172
  19.3 16.3 %collective-permute-start.8 = (bf16[128,2176]{1,0:T(8,128)(2,1)S(1)}, bf16[128,2176]{1,0:T(8,128)(2,1)S(1)}, u32[]{:S(2)}, u32[]{:S(2)}) collective-permute-start(bf16[128,2176]{1,0:T(8,128)(2,1)S(1)} %get-tuple-element.121.refs_5_.refs_14_), channel_id=1, source_target_pairs={{24,0},{28,4},{0,8},{4,12},{8,16},{12,20},{16,24},{20,28},{56,32},... | collective-permute-start | bytes 1671176 | tf_op jit(solution)/shard_map/ppermute | solution.py:31
  21.0 15.4 %collective-permute-start.6 = (bf16[128,2176]{1,0:T(8,128)(2,1)S(1)}, bf16[128,2176]{1,0:T(8,128)(2,1)S(1)}, u32[]{:S(2)}, u32[]{:S(2)}) collective-permute-start(bf16[128,2176]{1,0:T(8,128)(2,1)S(1)} %get-tuple-element.121.refs_5_.refs_14_), channel_id=1, source_target_pairs={{8,0},{12,4},{16,8},{20,12},{24,16},{28,20},{0,24},{4,28},{40,32},... | collective-permute-start | bytes 1671176 | tf_op jit(solution)/shard_map/ppermute | solution.py:31
  23.2 16.7 %collective-permute-start.5 = (bf16[128,2176]{1,0:T(8,128)(2,1)S(1)}, bf16[128,2176]{1,0:T(8,128)(2,1)S(1)}, u32[]{:S(2)}, u32[]{:S(2)}) collective-permute-start(bf16[128,2176]{1,0:T(8,128)(2,1)S(1)} %get-tuple-element.122.refs_0_.refs_10_), channel_id=1, source_target_pairs={{96,0},{100,4},{104,8},{108,12},{112,16},{116,20},{120,24},{124,28... | collective-permute-start | bytes 1671176 | tf_op jit(solution)/shard_map/ppermute | solution.py:31
  24.4 17.5 %collective-permute-start.3 = (bf16[128,2176]{1,0:T(8,128)(2,1)S(1)}, bf16[128,2176]{1,0:T(8,128)(2,1)S(1)}, u32[]{:S(2)}, u32[]{:S(2)}) collective-permute-start(bf16[128,2176]{1,0:T(8,128)(2,1)S(1)} %get-tuple-element.122.refs_0_.refs_10_), channel_id=1, source_target_pairs={{32,0},{36,4},{40,8},{44,12},{48,16},{52,20},{56,24},{60,28},{64,3... | collective-permute-start | bytes 1671176 | tf_op jit(solution)/shard_map/ppermute | solution.py:31
  36.4 8.7 %collective-permute-start.10 = (bf16[64,2176]{1,0:T(8,128)(2,1)}, bf16[64,2176]{1,0:T(8,128)(2,1)}, u32[]{:S(2)}, u32[]{:S(2)}) collective-permute-start(bf16[64,2176]{1,0:T(8,128)(2,1)} %slice.158), channel_id=1, source_target_pairs={{24,0},{28,4},{0,8},{4,12},{8,16},{12,20},{16,24},{20,28},{56,32},... | collective-permute-start | bytes 835592 | tf_op jit(solution)/shard_map/ppermute | solution.py:31
  37.2 7.8 %collective-permute-start.7 = (bf16[64,2176]{1,0:T(8,128)(2,1)}, bf16[64,2176]{1,0:T(8,128)(2,1)}, u32[]{:S(2)}, u32[]{:S(2)}) collective-permute-start(bf16[64,2176]{1,0:T(8,128)(2,1)} %slice.152), channel_id=1, source_target_pairs={{8,0},{12,4},{16,8},{20,12},{24,16},{28,20},{0,24},{4,28},{40,32},... | collective-permute-start | bytes 835592 | tf_op jit(solution)/shard_map/ppermute | solution.py:31
  40.7 8.1 %collective-permute-start.9 = (bf16[64,2176]{1,0:T(8,128)(2,1)}, bf16[64,2176]{1,0:T(8,128)(2,1)}, u32[]{:S(2)}, u32[]{:S(2)}) collective-permute-start(bf16[64,2176]{1,0:T(8,128)(2,1)} %slice.157), channel_id=1, source_target_pairs={{96,0},{100,4},{104,8},{108,12},{112,16},{116,20},{120,24},{124,28... | collective-permute-start | bytes 835592 | tf_op jit(solution)/shard_map/ppermute | solution.py:31
  42.7 6.6 %collective-permute-start.4 = (bf16[64,2176]{1,0:T(8,128)(2,1)}, bf16[64,2176]{1,0:T(8,128)(2,1)}, u32[]{:S(2)}, u32[]{:S(2)}) collective-permute-start(bf16[64,2176]{1,0:T(8,128)(2,1)} %slice.143), channel_id=1, source_target_pairs={{32,0},{36,4},{40,8},{44,12},{48,16},{52,20},{56,24},{60,28},{64,3... | collective-permute-start | bytes 835592 | tf_op jit(solution)/shard_map/ppermute | solution.py:31
  58.0 16.7 %collective-permute-start.11 = (bf16[2,96,2048]{2,1,0:T(8,128)(2,1)}, bf16[2,96,2048]{2,1,0:T(8,128)(2,1)S(1)}, u32[]{:S(2)}, u32[]{:S(2)}) collective-permute-start(bf16[2,96,2048]{2,1,0:T(8,128)(2,1)} %get-tuple-element.52), channel_id=1, source_target_pairs={{8,0},{12,4},{16,8},{20,12},{24,16},{28,20},{0,24},{4,28},{40,32},... | collective-permute-start | bytes 2359304 | tf_op jit(solution)/shard_map/ppermute | solution.py:31
  58.1 18.1 %collective-permute-start.12 = (bf16[2,96,2048]{2,1,0:T(8,128)(2,1)}, bf16[2,96,2048]{2,1,0:T(8,128)(2,1)S(1)}, u32[]{:S(2)}, u32[]{:S(2)}) collective-permute-start(bf16[2,96,2048]{2,1,0:T(8,128)(2,1)} %get-tuple-element.53), channel_id=1, source_target_pairs={{16,0},{20,4},{24,8},{28,12},{0,16},{4,20},{8,24},{12,28},{48,32},... | collective-permute-start | bytes 2359304 | tf_op jit(solution)/shard_map/ppermute | solution.py:31
  58.9 37.4 %collective-permute-start.13 = (bf16[2,96,2048]{2,1,0:T(8,128)(2,1)}, bf16[2,96,2048]{2,1,0:T(8,128)(2,1)S(1)}, u32[]{:S(2)}, u32[]{:S(2)}) collective-permute-start(bf16[2,96,2048]{2,1,0:T(8,128)(2,1)} %get-tuple-element.54), channel_id=1, source_target_pairs={{24,0},{28,4},{0,8},{4,12},{8,16},{12,20},{16,24},{20,28},{56,32},... | collective-permute-start | bytes 2359304 | tf_op jit(solution)/shard_map/ppermute | solution.py:31
  59.5 39.8 %collective-permute-start.14 = (bf16[2,96,2048]{2,1,0:T(8,128)(2,1)}, bf16[2,96,2048]{2,1,0:T(8,128)(2,1)}, u32[]{:S(2)}, u32[]{:S(2)}) collective-permute-start(bf16[2,96,2048]{2,1,0:T(8,128)(2,1)} %get-tuple-element.56), channel_id=1, source_target_pairs={{32,0},{36,4},{40,8},{44,12},{48,16},{52,20},{56,24},{60,28},{64,3... | collective-permute-start | bytes 2359304 | tf_op jit(solution)/shard_map/ppermute | solution.py:31
  62.2 38.4 %collective-permute-start.15 = (bf16[2,96,2048]{2,1,0:T(8,128)(2,1)}, bf16[2,96,2048]{2,1,0:T(8,128)(2,1)}, u32[]{:S(2)}, u32[]{:S(2)}) collective-permute-start(bf16[2,96,2048]{2,1,0:T(8,128)(2,1)} %get-tuple-element.57), channel_id=1, source_target_pairs={{64,0},{68,4},{72,8},{76,12},{80,16},{84,20},{88,24},{92,28},{96,3... | collective-permute-start | bytes 2359304 | tf_op jit(solution)/shard_map/ppermute | solution.py:31
  74.7 47.8 %copy-start.8 = (bf16[2,96,2048]{2,1,0:T(8,128)(2,1)}, bf16[2,96,2048]{2,1,0:T(8,128)(2,1)S(1)}, u32[]{:S(2)}) copy-start(bf16[2,96,2048]{2,1,0:T(8,128)(2,1)S(1)} %collective-permute-done.11.refs_1_) | copy-start | bytes 2359300
  74.7 25.9 %collective-permute-start.16 = (bf16[2,96,2048]{2,1,0:T(8,128)(2,1)}, bf16[2,96,2048]{2,1,0:T(8,128)(2,1)}, u32[]{:S(2)}, u32[]{:S(2)}) collective-permute-start(bf16[2,96,2048]{2,1,0:T(8,128)(2,1)} %get-tuple-element.58), channel_id=1, source_target_pairs={{96,0},{100,4},{104,8},{108,12},{112,16},{116,20},{120,24},{124,28... | collective-permute-start | bytes 2359304 | tf_op jit(solution)/shard_map/ppermute | solution.py:31
  76.2 46.3 %copy-start.9 = (bf16[2,96,2048]{2,1,0:T(8,128)(2,1)}, bf16[2,96,2048]{2,1,0:T(8,128)(2,1)S(1)}, u32[]{:S(2)}) copy-start(bf16[2,96,2048]{2,1,0:T(8,128)(2,1)S(1)} %collective-permute-done.12.refs_2_) | copy-start | bytes 2359300
  76.2 24.6 %collective-permute-start.20 = (bf16[2,96,2048]{2,1,0:T(8,128)(2,1)}, bf16[2,96,2048]{2,1,0:T(8,128)(2,1)S(1)}, u32[]{:S(2)}, u32[]{:S(2)}) collective-permute-start(bf16[2,96,2048]{2,1,0:T(8,128)(2,1)} %get-tuple-element.63), channel_id=1, source_target_pairs={{4,0},{0,4},{12,8},{8,12},{20,16},{16,20},{28,24},{24,28},{36,32},... | collective-permute-start | bytes 2359304 | tf_op jit(solution)/shard_map/ppermute | solution.py:31
  97.2 20.4 %collective-permute-start.21 = (bf16[2,96,2048]{2,1,0:T(8,128)(2,1)}, bf16[2,96,2048]{2,1,0:T(8,128)(2,1)S(1)}, u32[]{:S(2)}, u32[]{:S(2)}) collective-permute-start(bf16[2,96,2048]{2,1,0:T(8,128)(2,1)} %get-tuple-element.64), channel_id=1, source_target_pairs={{12,0},{8,4},{20,8},{16,12},{28,16},{24,20},{4,24},{0,28},{44,32},... | collective-permute-start | bytes 2359304 | tf_op jit(solution)/shard_map/ppermute | solution.py:31
  99.3 41.7 %collective-permute-start.22 = (bf16[2,96,2048]{2,1,0:T(8,128)(2,1)}, bf16[2,96,2048]{2,1,0:T(8,128)(2,1)}, u32[]{:S(2)}, u32[]{:S(2)}) collective-permute-start(bf16[2,96,2048]{2,1,0:T(8,128)(2,1)} %get-tuple-element.65), channel_id=1, source_target_pairs={{20,0},{16,4},{28,8},{24,12},{4,16},{0,20},{12,24},{8,28},{52,32},... | collective-permute-start | bytes 2359304 | tf_op jit(solution)/shard_map/ppermute | solution.py:31
  100.6 41.9 %collective-permute-start.23 = (bf16[2,96,2048]{2,1,0:T(8,128)(2,1)}, bf16[2,96,2048]{2,1,0:T(8,128)(2,1)}, u32[]{:S(2)}, u32[]{:S(2)}) collective-permute-start(bf16[2,96,2048]{2,1,0:T(8,128)(2,1)} %get-tuple-element.66), channel_id=1, source_target_pairs={{28,0},{24,4},{4,8},{0,12},{12,16},{8,20},{20,24},{16,28},{60,32},... | collective-permute-start | bytes 2359304 | tf_op jit(solution)/shard_map/ppermute | solution.py:31
  100.6 43.7 %collective-permute-start.24 = (bf16[2,96,2048]{2,1,0:T(8,128)(2,1)}, bf16[2,96,2048]{2,1,0:T(8,128)(2,1)}, u32[]{:S(2)}, u32[]{:S(2)}) collective-permute-start(bf16[2,96,2048]{2,1,0:T(8,128)(2,1)} %get-tuple-element.67), channel_id=1, source_target_pairs={{4,0},{0,4},{12,8},{8,12},{20,16},{16,20},{28,24},{24,28},{36,32},... | collective-permute-start | bytes 2359304 | tf_op jit(solution)/shard_map/ppermute | solution.py:31
  100.8 40.2 %copy-start.6 = (bf16[2,96,2048]{2,1,0:T(8,128)(2,1)}, bf16[2,96,2048]{2,1,0:T(8,128)(2,1)S(1)}, u32[]{:S(2)}) copy-start(bf16[2,96,2048]{2,1,0:T(8,128)(2,1)S(1)} %collective-permute-done.20.refs_0_) | copy-start | bytes 2359300
  100.8 43.4 %collective-permute-start.25 = (bf16[2,96,2048]{2,1,0:T(8,128)(2,1)}, bf16[2,96,2048]{2,1,0:T(8,128)(2,1)}, u32[]{:S(2)}, u32[]{:S(2)}) collective-permute-start(bf16[2,96,2048]{2,1,0:T(8,128)(2,1)} %get-tuple-element.68), channel_id=1, source_target_pairs={{36,0},{32,4},{44,8},{40,12},{52,16},{48,20},{60,24},{56,28},{68,3... | collective-permute-start | bytes 2359304 | tf_op jit(solution)/shard_map/ppermute | solution.py:31
  117.6 23.4 %copy-start.7 = (bf16[2,96,2048]{2,1,0:T(8,128)(2,1)}, bf16[2,96,2048]{2,1,0:T(8,128)(2,1)S(1)}, u32[]{:S(2)}) copy-start(bf16[2,96,2048]{2,1,0:T(8,128)(2,1)S(1)} %collective-permute-done.21.refs_1_) | copy-start | bytes 2359300
  117.6 27.3 %collective-permute-start.26 = (bf16[2,96,2048]{2,1,0:T(8,128)(2,1)}, bf16[2,96,2048]{2,1,0:T(8,128)(2,1)}, u32[]{:S(2)}, u32[]{:S(2)}) collective-permute-start(bf16[2,96,2048]{2,1,0:T(8,128)(2,1)} %get-tuple-element.69), channel_id=1, source_target_pairs={{68,0},{64,4},{76,8},{72,12},{84,16},{80,20},{92,24},{88,28},{100,... | collective-permute-start | bytes 2359304 | tf_op jit(solution)/shard_map/ppermute | solution.py:31
  141.0 21.5 %collective-permute-start.27 = (bf16[2,96,2048]{2,1,0:T(8,128)(2,1)}, bf16[2,96,2048]{2,1,0:T(8,128)(2,1)S(1)}, u32[]{:S(2)}, u32[]{:S(2)}) collective-permute-start(bf16[2,96,2048]{2,1,0:T(8,128)(2,1)} %get-tuple-element.70), channel_id=1, source_target_pairs={{100,0},{96,4},{108,8},{104,12},{116,16},{112,20},{124,24},{120,28... | collective-permute-start | bytes 2359304 | tf_op jit(solution)/shard_map/ppermute | solution.py:31
  142.5 39.5 %collective-permute-start.17 = (bf16[2,96,2048]{2,1,0:T(8,128)(2,1)}, bf16[2,96,2048]{2,1,0:T(8,128)(2,1)S(1)}, u32[]{:S(2)}, u32[]{:S(2)}) collective-permute-start(bf16[2,96,2048]{2,1,0:T(8,128)(2,1)} %get-tuple-element.60), channel_id=1, source_target_pairs={{8,0},{12,4},{16,8},{20,12},{24,16},{28,20},{0,24},{4,28},{40,32},... | collective-permute-start | bytes 2359304 | tf_op jit(solution)/shard_map/ppermute | solution.py:31
  144.3 37.8 %collective-permute-start.18 = (bf16[2,96,2048]{2,1,0:T(8,128)(2,1)}, bf16[2,96,2048]{2,1,0:T(8,128)(2,1)S(1)}, u32[]{:S(2)}, u32[]{:S(2)}) collective-permute-start(bf16[2,96,2048]{2,1,0:T(8,128)(2,1)} %get-tuple-element.61), channel_id=1, source_target_pairs={{16,0},{20,4},{24,8},{28,12},{0,16},{4,20},{8,24},{12,28},{48,32},... | collective-permute-start | bytes 2359304 | tf_op jit(solution)/shard_map/ppermute | solution.py:31
  144.3 38.3 %collective-permute-start.19 = (bf16[2,96,2048]{2,1,0:T(8,128)(2,1)}, bf16[2,96,2048]{2,1,0:T(8,128)(2,1)S(1)}, u32[]{:S(2)}, u32[]{:S(2)}) collective-permute-start(bf16[2,96,2048]{2,1,0:T(8,128)(2,1)} %get-tuple-element.62), channel_id=1, source_target_pairs={{24,0},{28,4},{0,8},{4,12},{8,16},{12,20},{16,24},{20,28},{56,32},... | collective-permute-start | bytes 2359304 | tf_op jit(solution)/shard_map/ppermute | solution.py:31
  144.9 39.1 %collective-permute-start.32 = (bf16[2,96,2048]{2,1,0:T(8,128)(2,1)}, bf16[2,96,2048]{2,1,0:T(8,128)(2,1)}, u32[]{:S(2)}, u32[]{:S(2)}) collective-permute-start(bf16[2,96,2048]{2,1,0:T(8,128)(2,1)} %get-tuple-element.76), channel_id=1, source_target_pairs={{32,0},{36,4},{40,8},{44,12},{48,16},{52,20},{56,24},{60,28},{64,3... | collective-permute-start | bytes 2359304 | tf_op jit(solution)/shard_map/ppermute | solution.py:31
  162.6 22.4 %collective-permute-start.33 = (bf16[2,96,2048]{2,1,0:T(8,128)(2,1)}, bf16[2,96,2048]{2,1,0:T(8,128)(2,1)}, u32[]{:S(2)}, u32[]{:S(2)}) collective-permute-start(bf16[2,96,2048]{2,1,0:T(8,128)(2,1)} %get-tuple-element.77), channel_id=1, source_target_pairs={{64,0},{68,4},{72,8},{76,12},{80,16},{84,20},{88,24},{92,28},{96,3... | collective-permute-start | bytes 2359304 | tf_op jit(solution)/shard_map/ppermute | solution.py:31
  182.0 40.7 %copy-start.12 = (bf16[2,96,2048]{2,1,0:T(8,128)(2,1)}, bf16[2,96,2048]{2,1,0:T(8,128)(2,1)S(1)}, u32[]{:S(2)}) copy-start(bf16[2,96,2048]{2,1,0:T(8,128)(2,1)S(1)} %collective-permute-done.17.refs_3_) | copy-start | bytes 2359300
  182.0 20.4 %collective-permute-start.34 = (bf16[2,96,2048]{2,1,0:T(8,128)(2,1)}, bf16[2,96,2048]{2,1,0:T(8,128)(2,1)S(1)}, u32[]{:S(2)}, u32[]{:S(2)}) collective-permute-start(bf16[2,96,2048]{2,1,0:T(8,128)(2,1)} %get-tuple-element.78), channel_id=1, source_target_pairs={{96,0},{100,4},{104,8},{108,12},{112,16},{116,20},{120,24},{124,28... | collective-permute-start | bytes 2359304 | tf_op jit(solution)/shard_map/ppermute | solution.py:31
  182.1 41.1 %copy-start.13 = (bf16[2,96,2048]{2,1,0:T(8,128)(2,1)}, bf16[2,96,2048]{2,1,0:T(8,128)(2,1)S(1)}, u32[]{:S(2)}) copy-start(bf16[2,96,2048]{2,1,0:T(8,128)(2,1)S(1)} %collective-permute-done.18.refs_4_) | copy-start | bytes 2359300
  182.1 21.3 %collective-permute-start.28 = (bf16[2,96,2048]{2,1,0:T(8,128)(2,1)}, bf16[2,96,2048]{2,1,0:T(8,128)(2,1)S(1)}, u32[]{:S(2)}, u32[]{:S(2)}) collective-permute-start(bf16[2,96,2048]{2,1,0:T(8,128)(2,1)} %get-tuple-element.71), channel_id=1, source_target_pairs={{4,0},{0,4},{12,8},{8,12},{20,16},{16,20},{28,24},{24,28},{36,32},... | collective-permute-start | bytes 2359304 | tf_op jit(solution)/shard_map/ppermute | solution.py:31
  182.6 41.2 %copy-start.14 = (bf16[2,96,2048]{2,1,0:T(8,128)(2,1)}, bf16[2,96,2048]{2,1,0:T(8,128)(2,1)S(1)}, u32[]{:S(2)}) copy-start(bf16[2,96,2048]{2,1,0:T(8,128)(2,1)S(1)} %collective-permute-done.19.refs_5_) | copy-start | bytes 2359300
  182.6 20.9 %collective-permute-start.29 = (bf16[2,96,2048]{2,1,0:T(8,128)(2,1)}, bf16[2,96,2048]{2,1,0:T(8,128)(2,1)S(1)}, u32[]{:S(2)}, u32[]{:S(2)}) collective-permute-start(bf16[2,96,2048]{2,1,0:T(8,128)(2,1)} %get-tuple-element.72), channel_id=1, source_target_pairs={{12,0},{8,4},{20,8},{16,12},{28,16},{24,20},{4,24},{0,28},{44,32},... | collective-permute-start | bytes 2359304 | tf_op jit(solution)/shard_map/ppermute | solution.py:31
  184.1 37.8 %collective-permute-start.30 = (bf16[2,96,2048]{2,1,0:T(8,128)(2,1)}, bf16[2,96,2048]{2,1,0:T(8,128)(2,1)S(1)}, u32[]{:S(2)}, u32[]{:S(2)}) collective-permute-start(bf16[2,96,2048]{2,1,0:T(8,128)(2,1)} %get-tuple-element.73), channel_id=1, source_target_pairs={{20,0},{16,4},{28,8},{24,12},{4,16},{0,20},{12,24},{8,28},{52,32},... | collective-permute-start | bytes 2359304 | tf_op jit(solution)/shard_map/ppermute | solution.py:31
  185.0 47.4 %collective-permute-start.31 = (bf16[2,96,2048]{2,1,0:T(8,128)(2,1)}, bf16[2,96,2048]{2,1,0:T(8,128)(2,1)}, u32[]{:S(2)}, u32[]{:S(2)}) collective-permute-start(bf16[2,96,2048]{2,1,0:T(8,128)(2,1)} %get-tuple-element.74), channel_id=1, source_target_pairs={{28,0},{24,4},{4,8},{0,12},{12,16},{8,20},{20,24},{16,28},{60,32},... | collective-permute-start | bytes 2359304 | tf_op jit(solution)/shard_map/ppermute | solution.py:31
  202.4 30.0 %collective-permute-start.35 = (bf16[2,96,2048]{2,1,0:T(8,128)(2,1)}, bf16[2,96,2048]{2,1,0:T(8,128)(2,1)}, u32[]{:S(2)}, u32[]{:S(2)}) collective-permute-start(bf16[2,96,2048]{2,1,0:T(8,128)(2,1)} %get-tuple-element.79), channel_id=1, source_target_pairs={{4,0},{0,4},{12,8},{8,12},{20,16},{16,20},{28,24},{24,28},{36,32},... | collective-permute-start | bytes 2359304 | tf_op jit(solution)/shard_map/ppermute | solution.py:31
  203.5 28.9 %collective-permute-start.36 = (bf16[2,96,2048]{2,1,0:T(8,128)(2,1)}, bf16[2,96,2048]{2,1,0:T(8,128)(2,1)}, u32[]{:S(2)}, u32[]{:S(2)}) collective-permute-start(bf16[2,96,2048]{2,1,0:T(8,128)(2,1)} %get-tuple-element.80), channel_id=1, source_target_pairs={{36,0},{32,4},{44,8},{40,12},{52,16},{48,20},{60,24},{56,28},{68,3... | collective-permute-start | bytes 2359304 | tf_op jit(solution)/shard_map/ppermute | solution.py:31
  203.5 36.8 %collective-permute-start.37 = (bf16[2,96,2048]{2,1,0:T(8,128)(2,1)}, bf16[2,96,2048]{2,1,0:T(8,128)(2,1)}, u32[]{:S(2)}, u32[]{:S(2)}) collective-permute-start(bf16[2,96,2048]{2,1,0:T(8,128)(2,1)} %get-tuple-element.81), channel_id=1, source_target_pairs={{68,0},{64,4},{76,8},{72,12},{84,16},{80,20},{92,24},{88,28},{100,... | collective-permute-start | bytes 2359304 | tf_op jit(solution)/shard_map/ppermute | solution.py:31
  222.8 34.3 %collective-permute-start.38 = (bf16[2,96,2048]{2,1,0:T(8,128)(2,1)}, bf16[2,96,2048]{2,1,0:T(8,128)(2,1)}, u32[]{:S(2)}, u32[]{:S(2)}) collective-permute-start(bf16[2,96,2048]{2,1,0:T(8,128)(2,1)} %get-tuple-element.82), channel_id=1, source_target_pairs={{100,0},{96,4},{108,8},{104,12},{116,16},{112,20},{124,24},{120,28... | collective-permute-start | bytes 2359304 | tf_op jit(solution)/shard_map/ppermute | solution.py:31
  265.8 38.1 %copy-start.19 = (bf16[128,2048]{1,0:T(8,128)(2,1)S(1)}, bf16[128,2048]{1,0:T(8,128)(2,1)}, u32[]{:S(2)}) copy-start(bf16[128,2048]{1,0:T(8,128)(2,1)} %get-tuple-element.90) | copy-start | bytes 1572868
  265.9 9.0 %collective-permute-start.39 = (bf16[64,2048]{1,0:T(8,128)(2,1)}, bf16[64,2048]{1,0:T(8,128)(2,1)S(1)}, u32[]{:S(2)}, u32[]{:S(2)}) collective-permute-start(bf16[64,2048]{1,0:T(8,128)(2,1)} %get-tuple-element.85), channel_id=1, source_target_pairs={{96,0},{100,4},{104,8},{108,12},{112,16},{116,20},{120,24},{124,28... | collective-permute-start | bytes 786440 | tf_op jit(solution)/shard_map/ppermute | solution.py:31
  265.9 24.9 %collective-permute-start.41 = (bf16[64,2048]{1,0:T(8,128)(2,1)}, bf16[64,2048]{1,0:T(8,128)(2,1)S(1)}, u32[]{:S(2)}, u32[]{:S(2)}) collective-permute-start(bf16[64,2048]{1,0:T(8,128)(2,1)} %get-tuple-element.86), channel_id=1, source_target_pairs={{32,0},{36,4},{40,8},{44,12},{48,16},{52,20},{56,24},{60,28},{64,3... | collective-permute-start | bytes 786440 | tf_op jit(solution)/shard_map/ppermute | solution.py:31
  268.6 22.3 %collective-permute-start.42 = (bf16[64,2048]{1,0:T(8,128)(2,1)}, bf16[64,2048]{1,0:T(8,128)(2,1)S(1)}, u32[]{:S(2)}, u32[]{:S(2)}) collective-permute-start(bf16[64,2048]{1,0:T(8,128)(2,1)} %get-tuple-element.87), channel_id=1, source_target_pairs={{96,0},{100,4},{104,8},{108,12},{112,16},{116,20},{120,24},{124,28... | collective-permute-start | bytes 786440 | tf_op jit(solution)/shard_map/ppermute | solution.py:31
  268.6 10.9 %collective-permute-start.43 = (bf16[64,2048]{1,0:T(8,128)(2,1)}, bf16[64,2048]{1,0:T(8,128)(2,1)S(1)}, u32[]{:S(2)}, u32[]{:S(2)}) collective-permute-start(bf16[64,2048]{1,0:T(8,128)(2,1)} %get-tuple-element.89), channel_id=1, source_target_pairs={{32,0},{36,4},{40,8},{44,12},{48,16},{52,20},{56,24},{60,28},{64,3... | collective-permute-start | bytes 786440 | tf_op jit(solution)/shard_map/ppermute | solution.py:31
  271.3 11.8 %collective-permute-start.45 = (bf16[64,2048]{1,0:T(8,128)(2,1)}, bf16[64,2048]{1,0:T(8,128)(2,1)S(1)}, u32[]{:S(2)}, u32[]{:S(2)}) collective-permute-start(bf16[64,2048]{1,0:T(8,128)(2,1)} %get-tuple-element.92), channel_id=1, source_target_pairs={{24,0},{28,4},{0,8},{4,12},{8,16},{12,20},{16,24},{20,28},{56,32},... | collective-permute-start | bytes 786440 | tf_op jit(solution)/shard_map/ppermute | solution.py:31
  274.8 21.1 %collective-permute-start.47 = (bf16[64,2048]{1,0:T(8,128)(2,1)}, bf16[64,2048]{1,0:T(8,128)(2,1)S(1)}, u32[]{:S(2)}, u32[]{:S(2)}) collective-permute-start(bf16[64,2048]{1,0:T(8,128)(2,1)} %get-tuple-element.93), channel_id=1, source_target_pairs={{8,0},{12,4},{16,8},{20,12},{24,16},{28,20},{0,24},{4,28},{40,32},... | collective-permute-start | bytes 786440 | tf_op jit(solution)/shard_map/ppermute | solution.py:31
  279.5 8.8 %collective-permute-start.49 = (bf16[64,2048]{1,0:T(8,128)(2,1)}, bf16[64,2048]{1,0:T(8,128)(2,1)S(1)}, u32[]{:S(2)}, u32[]{:S(2)}) collective-permute-start(bf16[64,2048]{1,0:T(8,128)(2,1)} %get-tuple-element.96), channel_id=1, source_target_pairs={{8,0},{12,4},{16,8},{20,12},{24,16},{28,20},{0,24},{4,28},{40,32},... | collective-permute-start | bytes 786440 | tf_op jit(solution)/shard_map/ppermute | solution.py:31
  283.1 9.5 %collective-permute-start.40 = (bf16[64,2048]{1,0:T(8,128)(2,1)S(1)}, bf16[64,2048]{1,0:T(8,128)(2,1)S(1)}, u32[]{:S(2)}, u32[]{:S(2)}) collective-permute-start(bf16[64,2048]{1,0:T(8,128)(2,1)S(1)} %add_convert_fusion.8), channel_id=1, source_target_pairs={{96,0},{100,4},{104,8},{108,12},{112,16},{116,20},{120,24},{124,28... | collective-permute-start | bytes 786440 | tf_op jit(solution)/shard_map/ppermute | solution.py:31
  288.3 6.3 %collective-permute-start.44 = (bf16[64,2048]{1,0:T(8,128)(2,1)S(1)}, bf16[64,2048]{1,0:T(8,128)(2,1)S(1)}, u32[]{:S(2)}, u32[]{:S(2)}) collective-permute-start(bf16[64,2048]{1,0:T(8,128)(2,1)S(1)} %add_convert_fusion.6), channel_id=1, source_target_pairs={{32,0},{36,4},{40,8},{44,12},{48,16},{52,20},{56,24},{60,28},{64,3... | collective-permute-start | bytes 786440 | tf_op jit(solution)/shard_map/ppermute | solution.py:31
  290.8 7.3 %collective-permute-start.48 = (bf16[64,2048]{1,0:T(8,128)(2,1)}, bf16[64,2048]{1,0:T(8,128)(2,1)S(1)}, u32[]{:S(2)}, u32[]{:S(2)}) collective-permute-start(bf16[64,2048]{1,0:T(8,128)(2,1)} %get-tuple-element.94), channel_id=1, source_target_pairs={{24,0},{28,4},{0,8},{4,12},{8,16},{12,20},{16,24},{20,28},{56,32},... | collective-permute-start | bytes 786440 | tf_op jit(solution)/shard_map/ppermute | solution.py:31
  290.9 13.0 %collective-permute-start.46 = (bf16[64,2048]{1,0:T(8,128)(2,1)S(1)}, bf16[64,2048]{1,0:T(8,128)(2,1)S(1)}, u32[]{:S(2)}, u32[]{:S(2)}) collective-permute-start(bf16[64,2048]{1,0:T(8,128)(2,1)S(1)} %add_convert_fusion.4), channel_id=1, source_target_pairs={{24,0},{28,4},{0,8},{4,12},{8,16},{12,20},{16,24},{20,28},{56,32},... | collective-permute-start | bytes 786440 | tf_op jit(solution)/shard_map/ppermute | solution.py:31
  292.6 11.3 %collective-permute-start.50 = (bf16[64,2048]{1,0:T(8,128)(2,1)S(1)}, bf16[64,2048]{1,0:T(8,128)(2,1)S(1)}, u32[]{:S(2)}, u32[]{:S(2)}) collective-permute-start(bf16[64,2048]{1,0:T(8,128)(2,1)S(1)} %add_convert_fusion.2), channel_id=1, source_target_pairs={{8,0},{12,4},{16,8},{20,12},{24,16},{28,20},{0,24},{4,28},{40,32},... | collective-permute-start | bytes 786440 | tf_op jit(solution)/shard_map/ppermute | solution.py:31
  304.3 6.9 %collective-permute-start.52 = (bf16[128,1024]{1,0:T(8,128)(2,1)S(1)}, bf16[128,1024]{1,0:T(8,128)(2,1)S(1)}, u32[]{:S(2)}, u32[]{:S(2)}) collective-permute-start(bf16[128,1024]{1,0:T(8,128)(2,1)S(1)} %pad_maximum_fusion.2), channel_id=1, source_target_pairs={{2,0},{3,1},{0,2},{1,3},{6,4},{7,5},{4,6},{5,7},{10,8},{11,9},{8,1... | collective-permute-start | bytes 786440 | tf_op jit(solution)/shard_map/ppermute | solution.py:27
  304.7 13.9 %collective-permute-start.51 = (bf16[128,1024]{1,0:T(8,128)(2,1)S(1)}, bf16[128,1024]{1,0:T(8,128)(2,1)S(1)}, u32[]{:S(2)}, u32[]{:S(2)}) collective-permute-start(bf16[128,1024]{1,0:T(8,128)(2,1)S(1)} %pad_maximum_fusion.1), channel_id=1, source_target_pairs={{3,0},{0,1},{1,2},{2,3},{7,4},{4,5},{5,6},{6,7},{11,8},{8,9},{9,10... | collective-permute-start | bytes 786440 | tf_op jit(solution)/shard_map/ppermute | solution.py:27
  304.8 13.8 %collective-permute-start.53 = (bf16[128,1024]{1,0:T(8,128)(2,1)S(1)}, bf16[128,1024]{1,0:T(8,128)(2,1)S(1)}, u32[]{:S(2)}, u32[]{:S(2)}) collective-permute-start(bf16[128,1024]{1,0:T(8,128)(2,1)S(1)} %fusion.7), channel_id=1, source_target_pairs={{1,0},{2,1},{3,2},{0,3},{5,4},{6,5},{7,6},{4,7},{9,8},{10,9},{11,1... | collective-permute-start | bytes 786440 | tf_op jit(solution)/shard_map/ppermute | solution.py:27
  (10 other events, 102.4 us)
where the time goes:
time: 320 us; the launch traced here: 319 us
  waiting for transfers between devices  148 us (46%)
  starting transfers between devices  85 us (27%)
  Pallas kernels  54.5 us (17%)
  local copies, waits for them, and re-layouts  19.1 us (6%)
  other arithmetic  11.8 us (4%)
    ppermute x48, waiting for transfers between devices, recv(): return lax.ppermute(a, 'ep', pairs)  125 us
    ppermute x48, starting transfers between devices, recv(): return lax.ppermute(a, 'ep', pairs)  77.2 us
    pallas_call x2, Pallas kernels, experts(): call(experts_body, (2,), [pl.BlockSpec(memory_space=pltpu.SMEM)] + [hbm]...  37 us
    ppermute x6, waiting for transfers between devices, recv(): return lax.ppermute(a, 'etp', [((i + d) % SIDE, i) for i in range(SIDE)])  23.1 us
    pallas_call x1, Pallas kernels, combine(): call(combine_body, (K // COLS,), [PAIRS] * 2 + [ROWS] * 16, ([DENSE] + [P...  8.78 us
    pallas_call x1, Pallas kernels, select(): call(select_body, (K // COLS,), [pl.BlockSpec(memory_space=pltpu.SMEM)] +...  8.64 us
    ppermute x6, starting transfers between devices, recv(): return lax.ppermute(a, 'etp', [((i + d) % SIDE, i) for i in range(SIDE)])  7.75 us
  transfers between devices with their start and end apart: 54, of which 21 were waited for; matrix products, arithmetic and copies ran while one was open for 8% of the time, Pallas kernels for 12%

commit v1 on v0

--- a/solution.py
+++ b/solution.py
@@ -43,7 +43,7 @@
 
 
 PAIRS = pl.BlockSpec((2, 256, 768), lambda i: (0, 0, 0))
-COLS = 512
+COLS = 1024
 META = pl.BlockSpec((16, TOK), lambda i: (0, K // TOK))
 DENSE = pl.BlockSpec((TOK, COLS), lambda i: (0, i))
 PART = pl.BlockSpec((TOK // 2, COLS), lambda i: (0, i))
@@ -116,7 +116,7 @@
 
 def experts_body(y_ref, *refs):
     pieces, (wg, wu, wd), outs = refs[:8], refs[8:11], refs[11:19]
-    gate, up, down, lhs, acc, hs, hid, res, sems, out_sems = refs[19:]
+    gu, down, lhs, acc, hs, hid, res, sems, out_sems = refs[19:]
     e = pl.program_id(0)
     y = y_ref[0]
 
@@ -129,8 +129,8 @@
         for dy in range(SIDE):
             src = pl.ds(pl.multiple_of(lax.rem(y + dy, SIDE) * 1024 + n * F, 128), F)
             dst = pl.ds(n * K + dy * F, F)
-            copies.append(pltpu.make_async_copy(wg.at[k, src, :], gate.at[k, dst, :], sems.at[k, n * 12 + 4 + dy]))
-            copies.append(pltpu.make_async_copy(wu.at[k, src, :], up.at[k, dst, :], sems.at[k, n * 12 + 8 + dy]))
+            copies.append(pltpu.make_async_copy(wg.at[k, src, :], gu.at[0, k, dst, :], sems.at[k, n * 12 + 4 + dy]))
+            copies.append(pltpu.make_async_copy(wu.at[k, src, :], gu.at[1, k, dst, :], sems.at[k, n * 12 + 8 + dy]))
         return copies
 
     def start(k, n):
@@ -151,22 +151,21 @@
             for n in range(3):
                 start(k, n)
 
-    @pl.loop(0, 2)
-    def _(half):
-        for n in range(2):
-            @pl.when(half == n)
-            def _(n=n):
-                wait(n)
-        rows = pl.ds(pl.multiple_of(half * K, K), K)
-        for n, w in enumerate((gate, up)):
-            acc[half, :, n * FF:(n + 1) * FF] = dot(lhs[e, half], w[e, rows, :])
+    @pl.loop(0, 4)
+    def _(n):
+        half, kind = n // 2, n % 2
+        for k in range(2):
+            @pl.when(n == 2 * k)
+            def _(k=k):
+                wait(k)
+        acc[kind, half] = dot(lhs[e, half], gu[kind, e, pl.ds(pl.multiple_of(half * K, K), K), :])
 
     @pl.loop(0, SIDE * SIDE)
     def _(n):
         to = pl.ds(pl.multiple_of(n * CAP, 8), CAP)
         fro = pl.ds(pl.multiple_of(((n % SIDE) * SIDE + n // SIDE) * CAP, 8), CAP)
-        v = acc[1, to, :] + acc[0, fro, :]
-        g, u = v[:, :FF], v[:, FF:]
+        g = acc[0, 1, to, :] + acc[0, 0, fro, :]
+        u = acc[1, 1, to, :] + acc[1, 0, fro, :]
         hs[to, :] = g * (1.0 / (1.0 + jnp.exp(-g))) * u
 
     hid[0] = jnp.concatenate([hs[(j * SIDE + i) * CAP:(j * SIDE + i + 1) * CAP, :] for i in range(SIDE) for j in range(SIDE)], axis=0).astype(BF)
@@ -194,8 +193,8 @@
 
 def experts(y, a, b, wg, wu, wd):
     hbm = pl.BlockSpec(memory_space=pl.ANY)
-    scratch = [pltpu.VMEM((2, 2 * K, FF), BF), pltpu.VMEM((2, 2 * K, FF), BF), pltpu.VMEM((2, FF, 2 * K), BF), pltpu.VMEM((2, 2, 384, K), BF),
-               pltpu.VMEM((2, 384, 2 * FF), F32), pltpu.VMEM((384, FF), F32), pltpu.VMEM((2, 384, FF), BF), pltpu.VMEM((2, 2, 384, K), BF),
+    scratch = [pltpu.VMEM((2, 2, 2 * K, FF), BF), pltpu.VMEM((2, FF, 2 * K), BF), pltpu.VMEM((2, 2, 384, K), BF),
+               pltpu.VMEM((2, 2, 384, FF), F32), pltpu.VMEM((384, FF), F32), pltpu.VMEM((2, 384, FF), BF), pltpu.VMEM((2, 2, 384, K), BF),
                pltpu.SemaphoreType.DMA((2, 25)), pltpu.SemaphoreType.DMA((2, 8))]
     o = call(experts_body, (2,), [pl.BlockSpec(memory_space=pltpu.SMEM)] + [hbm] * 11, [hbm] * 8,
              [(2, 96, K)] * 8, scratch)(y, *a, *b, wg, wu, wd)

time: 320 us -> 320 us (level)
  transfers between devices with their start and end apart: 54 -> 54, of which waited for: 21 -> 22; matrix products, arithmetic and copies ran while one was open for 8% -> 8% of each run, Pallas kernels for 12% -> 12%
where the time goes in v1:
time: 320 us; the launch traced here: 319 us
  waiting for transfers between devices  149 us (47%)
  starting transfers between devices  84.3 us (26%)
  Pallas kernels  54.2 us (17%)
  local copies, waits for them, and re-layouts  19.1 us (6%)
  other arithmetic  11.8 us (4%)
    ppermute x48, waiting for transfers between devices, recv(): return lax.ppermute(a, 'ep', pairs)  126 us
    ppermute x48, starting transfers between devices, recv(): return lax.ppermute(a, 'ep', pairs)  76.6 us
    pallas_call x2, Pallas kernels, experts(): call(experts_body, (2,), [pl.BlockSpec(memory_space=pltpu.SMEM)] + [hbm]...  38.6 us
    ppermute x6, waiting for transfers between devices, recv(): return lax.ppermute(a, 'etp', [((i + d) % SIDE, i) for i in range(SIDE)])  23.1 us
    pallas_call x1, Pallas kernels, combine(): call(combine_body, (K // COLS,), [PAIRS] * 2 + [ROWS] * 16, ([DENSE] + [P...  8.03 us
    ppermute x6, starting transfers between devices, recv(): return lax.ppermute(a, 'etp', [((i + d) % SIDE, i) for i in range(SIDE)])  7.77 us
    pallas_call x1, Pallas kernels, select(): call(select_body, (K // COLS,), [pl.BlockSpec(memory_space=pltpu.SMEM)] +...  7.6 us
  transfers between devices with their start and end apart: 54, of which 22 were waited for; matrix products, arithmetic and copies ran while one was open for 8% of the time, Pallas kernels for 12%

profile of v1, /device:TPU:1, one launch (start us, length us, event | category | flops | bytes accessed | tf_op | source)
XLA Modules:
  0.0 319.2 jit_solution(11563066868628248078)
XLA Ops:
  0.0 3.6 %collective-permute-start = (bf16[128,1024]{1,0:T(8,128)(2,1)}, bf16[128,1024]{1,0:T(8,128)(2,1)S(1)}, u32[]{:S(2)}, u32[]{:S(2)}) collective-permute-start(bf16[128,1024]{1,0:T(8,128)(2,1)} %param.6), channel_id=1, source_target_pairs={{1,0},{2,1},{3,2},{0,3},{5,4},{6,5},{7,6},{4,7},{9,8},{10,9},{11,1... | collective-permute-start | bytes 786440 | tf_op jit(solution)/shard_map/ppermute | solution.py:27
  4.6 1.0 slice_dynamic-update-slice_fusion.6
  7.1 7.3 %collective-permute-done = bf16[128,1024]{1,0:T(8,128)(2,1)S(1)} collective-permute-done((bf16[128,1024]{1,0:T(8,128)(2,1)}, bf16[128,1024]{1,0:T(8,128)(2,1)S(1)}, u32[]{:S(2)}, u32[]{:S(2)}) %collective-permute-start) | collective-permute-done | bytes 262176 | tf_op jit(solution)/shard_map/ppermute | solution.py:27
  14.4 4.7 %collective-permute-done.2 = bf16[128,1024]{1,0:T(8,128)(2,1)S(1)} collective-permute-done((bf16[128,1024]{1,0:T(8,128)(2,1)}, bf16[128,1024]{1,0:T(8,128)(2,1)S(1)}, u32[]{:S(2)}, u32[]{:S(2)}) %collective-permute-start.2) | collective-permute-done | bytes 262176 | tf_op jit(solution)/shard_map/ppermute | solution.py:27
  19.3 1.7 collective-permute-start.8
  21.0 2.2 collective-permute-start.6
  23.2 1.2 collective-permute-start.5
  24.4 1.5 collective-permute-start.3
  25.8 9.8 %collective-permute-done.8.refs_9_.refs_17_ = bf16[128,2176]{1,0:T(8,128)(2,1)S(1)} collective-permute-done((bf16[128,2176]{1,0:T(8,128)(2,1)S(1)}, bf16[128,2176]{1,0:T(8,128)(2,1)S(1)}, u32[]{:S(2)}, u32[]{:S(2)}) %collective-permute-start.8) | collective-permute-done | bytes 557088 | tf_op jit(solution)/shard_map/ppermute | solution.py:31
  37.2 2.7 collective-permute-start.7
  40.7 1.2 collective-permute-start.9
  42.7 1.5 collective-permute-start.4
  45.0 3.8 %collective-permute-done.9.refs_3_ = bf16[64,2176]{1,0:T(8,128)(2,1)} collective-permute-done((bf16[64,2176]{1,0:T(8,128)(2,1)}, bf16[64,2176]{1,0:T(8,128)(2,1)}, u32[]{:S(2)}, u32[]{:S(2)}) %collective-permute-start.9) | collective-permute-done | bytes 278560 | tf_op jit(solution)/shard_map/ppermute | solution.py:31
  49.3 7.6 %shard_map.64 = (bf16[2,96,2048]{2,1,0:T(8,128)(2,1)}, bf16[2,96,2048]{2,1,0:T(8,128)(2,1)}, bf16[2,96,2048]{2,1,0:T(8,128)(2,1)}, bf16[2,96,2048]{2,1,0:T(8,128...) custom-call(s32[3]{0:T(128)} %pad_add_fusion.where, ...), custom_call_target="tpu_custom_call" | custom-call | tf_op jit(solution)/shard_map/pallas_call | solution.py:93
  58.5 2.7 collective-permute-start.14
  61.5 12.2 %collective-permute-done.11.refs_1_ = bf16[2,96,2048]{2,1,0:T(8,128)(2,1)S(1)} collective-permute-done((bf16[2,96,2048]{2,1,0:T(8,128)(2,1)}, bf16[2,96,2048]{2,1,0:T(8,128)(2,1)S(1)}, u32[]{:S(2)}, u32[]{:S(2)}) %collective-permute-start.11) | collective-permute-done | bytes 786464 | tf_op jit(solution)/shard_map/ppermute | solution.py:31
  73.7 1.2 collective-permute-start.16
  75.1 7.1 %collective-permute-start.20 = (bf16[2,96,2048]{2,1,0:T(8,128)(2,1)}, bf16[2,96,2048]{2,1,0:T(8,128)(2,1)S(1)}, u32[]{:S(2)}, u32[]{:S(2)}) collective-permute-start(bf16[2,96,2048]{2,1,0:T(8,128)(2,1)} %get-tuple-element.63), channel_id=1, source_target_pairs={{4,0},{0,4},{12,8},{8,12},{20,16},{16,20},{28,24},{24,28},{36,32},... | collective-permute-start | bytes 2359304 | tf_op jit(solution)/shard_map/ppermute | solution.py:31
  82.2 13.0 %collective-permute-done.13.refs_3_ = bf16[2,96,2048]{2,1,0:T(8,128)(2,1)S(1)} collective-permute-done((bf16[2,96,2048]{2,1,0:T(8,128)(2,1)}, bf16[2,96,2048]{2,1,0:T(8,128)(2,1)S(1)}, u32[]{:S(2)}, u32[]{:S(2)}) %collective-permute-start.13) | collective-permute-done | bytes 786464 | tf_op jit(solution)/shard_map/ppermute | solution.py:31
  95.2 0.9 copy-done.10
  96.2 1.1 collective-permute-start.21
  98.2 1.3 collective-permute-start.22
  99.8 3.7 %collective-permute-start.25 = (bf16[2,96,2048]{2,1,0:T(8,128)(2,1)}, bf16[2,96,2048]{2,1,0:T(8,128)(2,1)}, u32[]{:S(2)}, u32[]{:S(2)}) collective-permute-start(bf16[2,96,2048]{2,1,0:T(8,128)(2,1)} %get-tuple-element.68), channel_id=1, source_target_pairs={{36,0},{32,4},{44,8},{40,12},{52,16},{48,20},{60,24},{56,28},{68,3... | collective-permute-start | bytes 2359304 | tf_op jit(solution)/shard_map/ppermute | solution.py:31
  103.4 13.2 %collective-permute-done.21.refs_1_ = bf16[2,96,2048]{2,1,0:T(8,128)(2,1)S(1)} collective-permute-done((bf16[2,96,2048]{2,1,0:T(8,128)(2,1)}, bf16[2,96,2048]{2,1,0:T(8,128)(2,1)S(1)}, u32[]{:S(2)}, u32[]{:S(2)}) %collective-permute-start.21) | collective-permute-done | bytes 786464 | tf_op jit(solution)/shard_map/ppermute | solution.py:31
  116.6 2.1 collective-permute-start.26
  121.5 19.3 %shard_map.65 = (bf16[2,96,2048]{2,1,0:T(8,128)(2,1)}, bf16[2,96,2048]{2,1,0:T(8,128)(2,1)}, bf16[2,96,2048]{2,1,0:T(8,128)(2,1)}, bf16[2,96,2048]{2,1,0:T(8,128...) custom-call(s32[1]{0:T(128)} %bitcast.48.y_ref, ...), custom_call_target="tpu_custom_call" | custom-call | tf_op jit(solution)/shard_map/pallas_call | solution.py:199
  140.8 1.5 collective-permute-start.27
  142.2 1.8 collective-permute-start.17
  144.7 1.5 collective-permute-start.32
  147.7 14.6 %collective-permute-done.27.refs_7_ = bf16[2,96,2048]{2,1,0:T(8,128)(2,1)S(1)} collective-permute-done((bf16[2,96,2048]{2,1,0:T(8,128)(2,1)}, bf16[2,96,2048]{2,1,0:T(8,128)(2,1)S(1)}, u32[]{:S(2)}, u32[]{:S(2)}) %collective-permute-start.27) | collective-permute-done | bytes 786464 | tf_op jit(solution)/shard_map/ppermute | solution.py:31
  162.3 0.9 copy-done.11
  163.2 19.3 %shard_map.66 = (bf16[2,96,2048]{2,1,0:T(8,128)(2,1)}, bf16[2,96,2048]{2,1,0:T(8,128)(2,1)}, bf16[2,96,2048]{2,1,0:T(8,128)(2,1)}, bf16[2,96,2048]{2,1,0:T(8,128...) custom-call(s32[1]{0:T(128)} %bitcast.48.y_ref, ...), custom_call_target="tpu_custom_call" | custom-call | tf_op jit(solution)/shard_map/pallas_call | solution.py:199
  183.1 1.5 collective-permute-start.29
  185.4 1.0 collective-permute-start.31
  186.4 16.5 %collective-permute-done.34.refs_13_ = bf16[2,96,2048]{2,1,0:T(8,128)(2,1)S(1)} collective-permute-done((bf16[2,96,2048]{2,1,0:T(8,128)(2,1)}, bf16[2,96,2048]{2,1,0:T(8,128)(2,1)S(1)}, u32[]{:S(2)}, u32[]{:S(2)}) %collective-permute-start.34) | collective-permute-done | bytes 786464 | tf_op jit(solution)/shard_map/ppermute | solution.py:31
  202.9 1.1 collective-permute-start.35
  204.0 18.3 %collective-permute-start.37 = (bf16[2,96,2048]{2,1,0:T(8,128)(2,1)}, bf16[2,96,2048]{2,1,0:T(8,128)(2,1)}, u32[]{:S(2)}, u32[]{:S(2)}) collective-permute-start(bf16[2,96,2048]{2,1,0:T(8,128)(2,1)} %get-tuple-element.81), channel_id=1, source_target_pairs={{68,0},{64,4},{76,8},{72,12},{84,16},{80,20},{92,24},{88,28},{100,... | collective-permute-start | bytes 2359304 | tf_op jit(solution)/shard_map/ppermute | solution.py:31
  222.4 0.9 copy-done.18
  224.3 1.1 and.126
  227.0 1.1 and.135
  231.1 1.8 fusion.1
  232.9 7.9 %collective-permute-done.37.refs_16_ = bf16[2,96,2048]{2,1,0:T(8,128)(2,1)} collective-permute-done((bf16[2,96,2048]{2,1,0:T(8,128)(2,1)}, bf16[2,96,2048]{2,1,0:T(8,128)(2,1)}, u32[]{:S(2)}, u32[]{:S(2)}) %collective-permute-start.37) | collective-permute-done | bytes 786464 | tf_op jit(solution)/shard_map/ppermute | solution.py:31
  240.8 16.8 %collective-permute-done.38.refs_17_ = bf16[2,96,2048]{2,1,0:T(8,128)(2,1)} collective-permute-done((bf16[2,96,2048]{2,1,0:T(8,128)(2,1)}, bf16[2,96,2048]{2,1,0:T(8,128)(2,1)}, u32[]{:S(2)}, u32[]{:S(2)}) %collective-permute-start.38) | collective-permute-done | bytes 786464 | tf_op jit(solution)/shard_map/ppermute | solution.py:31
  257.6 8.0 %shard_map.67 = (bf16[128,2048]{1,0:T(8,128)(2,1)}, bf16[64,2048]{1,0:T(8,128)(2,1)}, bf16[64,2048]{1,0:T(8,128)(2,1)}, bf16[64,2048]{1,0:T(8,128)(2,1)}, bf16[6...) custom-call(bf16[2,256,768]{2,1,0:T(8,128)(2,1)} %get-tuple-element., ...), custom_call_target="tpu_custom_call" | custom-call | tf_op jit(solution)/shard_map/pallas_call | solution.py:114
  265.7 2.7 collective-permute-start.41
  268.4 2.7 collective-permute-start.43
  271.0 3.5 %collective-permute-done.39 = bf16[64,2048]{1,0:T(8,128)(2,1)S(1)} collective-permute-done((bf16[64,2048]{1,0:T(8,128)(2,1)}, bf16[64,2048]{1,0:T(8,128)(2,1)S(1)}, u32[]{:S(2)}, u32[]{:S(2)}) %collective-permute-start.39) | collective-permute-done | bytes 262176 | tf_op jit(solution)/shard_map/ppermute | solution.py:31
  274.6 2.6 collective-permute-start.47
  277.1 1.0 add_convert_fusion.8
  278.2 1.1 collective-permute-done.43
  279.3 2.6 collective-permute-start.49
  281.8 1.0 add_convert_fusion.6
  283.0 1.0 add_convert_fusion.4
  284.0 4.0 %collective-permute-done.49 = bf16[64,2048]{1,0:T(8,128)(2,1)S(1)} collective-permute-done((bf16[64,2048]{1,0:T(8,128)(2,1)}, bf16[64,2048]{1,0:T(8,128)(2,1)S(1)}, u32[]{:S(2)}, u32[]{:S(2)}) %collective-permute-start.49) | collective-permute-done | bytes 262176 | tf_op jit(solution)/shard_map/ppermute | solution.py:31
  288.0 1.5 collective-permute-start.44
  289.5 1.0 add_convert_fusion.2
  290.6 1.8 collective-permute-start.46
  292.4 1.7 collective-permute-start.50
  294.3 1.3 add_convert_fusion.7
  295.6 2.3 collective-permute-done.48
  297.9 5.8 %collective-permute-done.46 = bf16[64,2048]{1,0:T(8,128)(2,1)S(1)} collective-permute-done((bf16[64,2048]{1,0:T(8,128)(2,1)S(1)}, bf16[64,2048]{1,0:T(8,128)(2,1)S(1)}, u32[]{:S(2)}, u32[]{:S(2)}) %collective-permute-start.46) | collective-permute-done | bytes 262176 | tf_op jit(solution)/shard_map/ppermute | solution.py:31
  304.6 2.7 collective-permute-start.53
  307.2 3.7 %collective-permute-done.52 = bf16[128,1024]{1,0:T(8,128)(2,1)S(1)} collective-permute-done((bf16[128,1024]{1,0:T(8,128)(2,1)S(1)}, bf16[128,1024]{1,0:T(8,128)(2,1)S(1)}, u32[]{:S(2)}, u32[]{:S(2)}) %collective-permute-start.52) | collective-permute-done | bytes 262176 | tf_op jit(solution)/shard_map/ppermute | solution.py:27
  310.9 7.4 %collective-permute-done.51 = bf16[128,1024]{1,0:T(8,128)(2,1)S(1)} collective-permute-done((bf16[128,1024]{1,0:T(8,128)(2,1)S(1)}, bf16[128,1024]{1,0:T(8,128)(2,1)S(1)}, u32[]{:S(2)}, u32[]{:S(2)}) %collective-permute-start.51) | collective-permute-done | bytes 262176 | tf_op jit(solution)/shard_map/ppermute | solution.py:27
  (156 shorter events, 24.7 us)
Async XLA Ops:
  0.0 14.3 %collective-permute-start = (bf16[128,1024]{1,0:T(8,128)(2,1)}, bf16[128,1024]{1,0:T(8,128)(2,1)S(1)}, u32[]{:S(2)}, u32[]{:S(2)}) collective-permute-start(bf16[128,1024]{1,0:T(8,128)(2,1)} %param.6), channel_id=1, source_target_pairs={{1,0},{2,1},{3,2},{0,3},{5,4},{6,5},{7,6},{4,7},{9,8},{10,9},{11,1... | collective-permute-start | bytes 786440 | tf_op jit(solution)/shard_map/ppermute | solution.py:27
  3.6 10.8 %collective-permute-start.1 = (bf16[128,1024]{1,0:T(8,128)(2,1)}, bf16[128,1024]{1,0:T(8,128)(2,1)S(1)}, u32[]{:S(2)}, u32[]{:S(2)}) collective-permute-start(bf16[128,1024]{1,0:T(8,128)(2,1)} %param.6), channel_id=1, source_target_pairs={{2,0},{3,1},{0,2},{1,3},{6,4},{7,5},{4,6},{5,7},{10,8},{11,9},{8,1... | collective-permute-start | bytes 786440 | tf_op jit(solution)/shard_map/ppermute | solution.py:27
  3.9 15.2 %collective-permute-start.2 = (bf16[128,1024]{1,0:T(8,128)(2,1)}, bf16[128,1024]{1,0:T(8,128)(2,1)S(1)}, u32[]{:S(2)}, u32[]{:S(2)}) collective-permute-start(bf16[128,1024]{1,0:T(8,128)(2,1)} %param.6), channel_id=1, source_target_pairs={{3,0},{0,1},{1,2},{2,3},{7,4},{4,5},{5,6},{6,7},{11,8},{8,9},{9,10... | collective-permute-start | bytes 786440 | tf_op jit(solution)/shard_map/ppermute | solution.py:27
  19.2 30.1 %copy-start.4 = (bf16[128,2176]{1,0:T(8,128)(2,1)}, bf16[128,2176]{1,0:T(8,128)(2,1)S(1)}, u32[]{:S(2)}) copy-start(bf16[128,2176]{1,0:T(8,128)(2,1)S(1)} %get-tuple-element.121.refs_5_.refs_14_) | copy-start | bytes 1671172
  19.2 30.1 %copy-start.5 = (bf16[128,2176]{1,0:T(8,128)(2,1)}, bf16[128,2176]{1,0:T(8,128)(2,1)S(1)}, u32[]{:S(2)}) copy-start(bf16[128,2176]{1,0:T(8,128)(2,1)S(1)} %get-tuple-element.122.refs_0_.refs_10_) | copy-start | bytes 1671172
  19.3 16.3 %collective-permute-start.8 = (bf16[128,2176]{1,0:T(8,128)(2,1)S(1)}, bf16[128,2176]{1,0:T(8,128)(2,1)S(1)}, u32[]{:S(2)}, u32[]{:S(2)}) collective-permute-start(bf16[128,2176]{1,0:T(8,128)(2,1)S(1)} %get-tuple-element.121.refs_5_.refs_14_), channel_id=1, source_target_pairs={{24,0},{28,4},{0,8},{4,12},{8,16},{12,20},{16,24},{20,28},{56,32},... | collective-permute-start | bytes 1671176 | tf_op jit(solution)/shard_map/ppermute | solution.py:31
  21.0 15.4 %collective-permute-start.6 = (bf16[128,2176]{1,0:T(8,128)(2,1)S(1)}, bf16[128,2176]{1,0:T(8,128)(2,1)S(1)}, u32[]{:S(2)}, u32[]{:S(2)}) collective-permute-start(bf16[128,2176]{1,0:T(8,128)(2,1)S(1)} %get-tuple-element.121.refs_5_.refs_14_), channel_id=1, source_target_pairs={{8,0},{12,4},{16,8},{20,12},{24,16},{28,20},{0,24},{4,28},{40,32},... | collective-permute-start | bytes 1671176 | tf_op jit(solution)/shard_map/ppermute | solution.py:31
  23.2 16.7 %collective-permute-start.5 = (bf16[128,2176]{1,0:T(8,128)(2,1)S(1)}, bf16[128,2176]{1,0:T(8,128)(2,1)S(1)}, u32[]{:S(2)}, u32[]{:S(2)}) collective-permute-start(bf16[128,2176]{1,0:T(8,128)(2,1)S(1)} %get-tuple-element.122.refs_0_.refs_10_), channel_id=1, source_target_pairs={{96,0},{100,4},{104,8},{108,12},{112,16},{116,20},{120,24},{124,28... | collective-permute-start | bytes 1671176 | tf_op jit(solution)/shard_map/ppermute | solution.py:31
  24.4 17.5 %collective-permute-start.3 = (bf16[128,2176]{1,0:T(8,128)(2,1)S(1)}, bf16[128,2176]{1,0:T(8,128)(2,1)S(1)}, u32[]{:S(2)}, u32[]{:S(2)}) collective-permute-start(bf16[128,2176]{1,0:T(8,128)(2,1)S(1)} %get-tuple-element.122.refs_0_.refs_10_), channel_id=1, source_target_pairs={{32,0},{36,4},{40,8},{44,12},{48,16},{52,20},{56,24},{60,28},{64,3... | collective-permute-start | bytes 1671176 | tf_op jit(solution)/shard_map/ppermute | solution.py:31
  36.4 8.7 %collective-permute-start.10 = (bf16[64,2176]{1,0:T(8,128)(2,1)}, bf16[64,2176]{1,0:T(8,128)(2,1)}, u32[]{:S(2)}, u32[]{:S(2)}) collective-permute-start(bf16[64,2176]{1,0:T(8,128)(2,1)} %slice.158), channel_id=1, source_target_pairs={{24,0},{28,4},{0,8},{4,12},{8,16},{12,20},{16,24},{20,28},{56,32},... | collective-permute-start | bytes 835592 | tf_op jit(solution)/shard_map/ppermute | solution.py:31
  37.2 7.8 %collective-permute-start.7 = (bf16[64,2176]{1,0:T(8,128)(2,1)}, bf16[64,2176]{1,0:T(8,128)(2,1)}, u32[]{:S(2)}, u32[]{:S(2)}) collective-permute-start(bf16[64,2176]{1,0:T(8,128)(2,1)} %slice.152), channel_id=1, source_target_pairs={{8,0},{12,4},{16,8},{20,12},{24,16},{28,20},{0,24},{4,28},{40,32},... | collective-permute-start | bytes 835592 | tf_op jit(solution)/shard_map/ppermute | solution.py:31
  40.7 8.1 %collective-permute-start.9 = (bf16[64,2176]{1,0:T(8,128)(2,1)}, bf16[64,2176]{1,0:T(8,128)(2,1)}, u32[]{:S(2)}, u32[]{:S(2)}) collective-permute-start(bf16[64,2176]{1,0:T(8,128)(2,1)} %slice.157), channel_id=1, source_target_pairs={{96,0},{100,4},{104,8},{108,12},{112,16},{116,20},{120,24},{124,28... | collective-permute-start | bytes 835592 | tf_op jit(solution)/shard_map/ppermute | solution.py:31
  42.7 6.6 %collective-permute-start.4 = (bf16[64,2176]{1,0:T(8,128)(2,1)}, bf16[64,2176]{1,0:T(8,128)(2,1)}, u32[]{:S(2)}, u32[]{:S(2)}) collective-permute-start(bf16[64,2176]{1,0:T(8,128)(2,1)} %slice.143), channel_id=1, source_target_pairs={{32,0},{36,4},{40,8},{44,12},{48,16},{52,20},{56,24},{60,28},{64,3... | collective-permute-start | bytes 835592 | tf_op jit(solution)/shard_map/ppermute | solution.py:31
  56.9 16.7 %collective-permute-start.11 = (bf16[2,96,2048]{2,1,0:T(8,128)(2,1)}, bf16[2,96,2048]{2,1,0:T(8,128)(2,1)S(1)}, u32[]{:S(2)}, u32[]{:S(2)}) collective-permute-start(bf16[2,96,2048]{2,1,0:T(8,128)(2,1)} %get-tuple-element.52), channel_id=1, source_target_pairs={{8,0},{12,4},{16,8},{20,12},{24,16},{28,20},{0,24},{4,28},{40,32},... | collective-permute-start | bytes 2359304 | tf_op jit(solution)/shard_map/ppermute | solution.py:31
  57.0 18.1 %collective-permute-start.12 = (bf16[2,96,2048]{2,1,0:T(8,128)(2,1)}, bf16[2,96,2048]{2,1,0:T(8,128)(2,1)S(1)}, u32[]{:S(2)}, u32[]{:S(2)}) collective-permute-start(bf16[2,96,2048]{2,1,0:T(8,128)(2,1)} %get-tuple-element.53), channel_id=1, source_target_pairs={{16,0},{20,4},{24,8},{28,12},{0,16},{4,20},{8,24},{12,28},{48,32},... | collective-permute-start | bytes 2359304 | tf_op jit(solution)/shard_map/ppermute | solution.py:31
  57.9 37.4 %collective-permute-start.13 = (bf16[2,96,2048]{2,1,0:T(8,128)(2,1)}, bf16[2,96,2048]{2,1,0:T(8,128)(2,1)S(1)}, u32[]{:S(2)}, u32[]{:S(2)}) collective-permute-start(bf16[2,96,2048]{2,1,0:T(8,128)(2,1)} %get-tuple-element.54), channel_id=1, source_target_pairs={{24,0},{28,4},{0,8},{4,12},{8,16},{12,20},{16,24},{20,28},{56,32},... | collective-permute-start | bytes 2359304 | tf_op jit(solution)/shard_map/ppermute | solution.py:31
  58.5 39.8 %collective-permute-start.14 = (bf16[2,96,2048]{2,1,0:T(8,128)(2,1)}, bf16[2,96,2048]{2,1,0:T(8,128)(2,1)}, u32[]{:S(2)}, u32[]{:S(2)}) collective-permute-start(bf16[2,96,2048]{2,1,0:T(8,128)(2,1)} %get-tuple-element.56), channel_id=1, source_target_pairs={{32,0},{36,4},{40,8},{44,12},{48,16},{52,20},{56,24},{60,28},{64,3... | collective-permute-start | bytes 2359304 | tf_op jit(solution)/shard_map/ppermute | solution.py:31
  61.2 38.4 %collective-permute-start.15 = (bf16[2,96,2048]{2,1,0:T(8,128)(2,1)}, bf16[2,96,2048]{2,1,0:T(8,128)(2,1)}, u32[]{:S(2)}, u32[]{:S(2)}) collective-permute-start(bf16[2,96,2048]{2,1,0:T(8,128)(2,1)} %get-tuple-element.57), channel_id=1, source_target_pairs={{64,0},{68,4},{72,8},{76,12},{80,16},{84,20},{88,24},{92,28},{96,3... | collective-permute-start | bytes 2359304 | tf_op jit(solution)/shard_map/ppermute | solution.py:31
  73.7 47.8 %copy-start.8 = (bf16[2,96,2048]{2,1,0:T(8,128)(2,1)}, bf16[2,96,2048]{2,1,0:T(8,128)(2,1)S(1)}, u32[]{:S(2)}) copy-start(bf16[2,96,2048]{2,1,0:T(8,128)(2,1)S(1)} %collective-permute-done.11.refs_1_) | copy-start | bytes 2359300
  73.7 25.9 %collective-permute-start.16 = (bf16[2,96,2048]{2,1,0:T(8,128)(2,1)}, bf16[2,96,2048]{2,1,0:T(8,128)(2,1)}, u32[]{:S(2)}, u32[]{:S(2)}) collective-permute-start(bf16[2,96,2048]{2,1,0:T(8,128)(2,1)} %get-tuple-element.58), channel_id=1, source_target_pairs={{96,0},{100,4},{104,8},{108,12},{112,16},{116,20},{120,24},{124,28... | collective-permute-start | bytes 2359304 | tf_op jit(solution)/shard_map/ppermute | solution.py:31
  75.1 46.3 %copy-start.9 = (bf16[2,96,2048]{2,1,0:T(8,128)(2,1)}, bf16[2,96,2048]{2,1,0:T(8,128)(2,1)S(1)}, u32[]{:S(2)}) copy-start(bf16[2,96,2048]{2,1,0:T(8,128)(2,1)S(1)} %collective-permute-done.12.refs_2_) | copy-start | bytes 2359300
  75.1 24.6 %collective-permute-start.20 = (bf16[2,96,2048]{2,1,0:T(8,128)(2,1)}, bf16[2,96,2048]{2,1,0:T(8,128)(2,1)S(1)}, u32[]{:S(2)}, u32[]{:S(2)}) collective-permute-start(bf16[2,96,2048]{2,1,0:T(8,128)(2,1)} %get-tuple-element.63), channel_id=1, source_target_pairs={{4,0},{0,4},{12,8},{8,12},{20,16},{16,20},{28,24},{24,28},{36,32},... | collective-permute-start | bytes 2359304 | tf_op jit(solution)/shard_map/ppermute | solution.py:31
  96.2 20.4 %collective-permute-start.21 = (bf16[2,96,2048]{2,1,0:T(8,128)(2,1)}, bf16[2,96,2048]{2,1,0:T(8,128)(2,1)S(1)}, u32[]{:S(2)}, u32[]{:S(2)}) collective-permute-start(bf16[2,96,2048]{2,1,0:T(8,128)(2,1)} %get-tuple-element.64), channel_id=1, source_target_pairs={{12,0},{8,4},{20,8},{16,12},{28,16},{24,20},{4,24},{0,28},{44,32},... | collective-permute-start | bytes 2359304 | tf_op jit(solution)/shard_map/ppermute | solution.py:31
  98.2 42.5 %collective-permute-start.22 = (bf16[2,96,2048]{2,1,0:T(8,128)(2,1)}, bf16[2,96,2048]{2,1,0:T(8,128)(2,1)}, u32[]{:S(2)}, u32[]{:S(2)}) collective-permute-start(bf16[2,96,2048]{2,1,0:T(8,128)(2,1)} %get-tuple-element.65), channel_id=1, source_target_pairs={{20,0},{16,4},{28,8},{24,12},{4,16},{0,20},{12,24},{8,28},{52,32},... | collective-permute-start | bytes 2359304 | tf_op jit(solution)/shard_map/ppermute | solution.py:31
  99.5 42.7 %collective-permute-start.23 = (bf16[2,96,2048]{2,1,0:T(8,128)(2,1)}, bf16[2,96,2048]{2,1,0:T(8,128)(2,1)}, u32[]{:S(2)}, u32[]{:S(2)}) collective-permute-start(bf16[2,96,2048]{2,1,0:T(8,128)(2,1)} %get-tuple-element.66), channel_id=1, source_target_pairs={{28,0},{24,4},{4,8},{0,12},{12,16},{8,20},{20,24},{16,28},{60,32},... | collective-permute-start | bytes 2359304 | tf_op jit(solution)/shard_map/ppermute | solution.py:31
  99.5 44.4 %collective-permute-start.24 = (bf16[2,96,2048]{2,1,0:T(8,128)(2,1)}, bf16[2,96,2048]{2,1,0:T(8,128)(2,1)}, u32[]{:S(2)}, u32[]{:S(2)}) collective-permute-start(bf16[2,96,2048]{2,1,0:T(8,128)(2,1)} %get-tuple-element.67), channel_id=1, source_target_pairs={{4,0},{0,4},{12,8},{8,12},{20,16},{16,20},{28,24},{24,28},{36,32},... | collective-permute-start | bytes 2359304 | tf_op jit(solution)/shard_map/ppermute | solution.py:31
  99.8 40.9 %copy-start.6 = (bf16[2,96,2048]{2,1,0:T(8,128)(2,1)}, bf16[2,96,2048]{2,1,0:T(8,128)(2,1)S(1)}, u32[]{:S(2)}) copy-start(bf16[2,96,2048]{2,1,0:T(8,128)(2,1)S(1)} %collective-permute-done.20.refs_0_) | copy-start | bytes 2359300
  99.8 44.2 %collective-permute-start.25 = (bf16[2,96,2048]{2,1,0:T(8,128)(2,1)}, bf16[2,96,2048]{2,1,0:T(8,128)(2,1)}, u32[]{:S(2)}, u32[]{:S(2)}) collective-permute-start(bf16[2,96,2048]{2,1,0:T(8,128)(2,1)} %get-tuple-element.68), channel_id=1, source_target_pairs={{36,0},{32,4},{44,8},{40,12},{52,16},{48,20},{60,24},{56,28},{68,3... | collective-permute-start | bytes 2359304 | tf_op jit(solution)/shard_map/ppermute | solution.py:31
  116.6 24.1 %copy-start.7 = (bf16[2,96,2048]{2,1,0:T(8,128)(2,1)}, bf16[2,96,2048]{2,1,0:T(8,128)(2,1)S(1)}, u32[]{:S(2)}) copy-start(bf16[2,96,2048]{2,1,0:T(8,128)(2,1)S(1)} %collective-permute-done.21.refs_1_) | copy-start | bytes 2359300
  116.6 28.1 %collective-permute-start.26 = (bf16[2,96,2048]{2,1,0:T(8,128)(2,1)}, bf16[2,96,2048]{2,1,0:T(8,128)(2,1)}, u32[]{:S(2)}, u32[]{:S(2)}) collective-permute-start(bf16[2,96,2048]{2,1,0:T(8,128)(2,1)} %get-tuple-element.69), channel_id=1, source_target_pairs={{68,0},{64,4},{76,8},{72,12},{84,16},{80,20},{92,24},{88,28},{100,... | collective-permute-start | bytes 2359304 | tf_op jit(solution)/shard_map/ppermute | solution.py:31
  140.8 21.6 %collective-permute-start.27 = (bf16[2,96,2048]{2,1,0:T(8,128)(2,1)}, bf16[2,96,2048]{2,1,0:T(8,128)(2,1)S(1)}, u32[]{:S(2)}, u32[]{:S(2)}) collective-permute-start(bf16[2,96,2048]{2,1,0:T(8,128)(2,1)} %get-tuple-element.70), channel_id=1, source_target_pairs={{100,0},{96,4},{108,8},{104,12},{116,16},{112,20},{124,24},{120,28... | collective-permute-start | bytes 2359304 | tf_op jit(solution)/shard_map/ppermute | solution.py:31
  142.2 40.3 %collective-permute-start.17 = (bf16[2,96,2048]{2,1,0:T(8,128)(2,1)}, bf16[2,96,2048]{2,1,0:T(8,128)(2,1)S(1)}, u32[]{:S(2)}, u32[]{:S(2)}) collective-permute-start(bf16[2,96,2048]{2,1,0:T(8,128)(2,1)} %get-tuple-element.60), channel_id=1, source_target_pairs={{8,0},{12,4},{16,8},{20,12},{24,16},{28,20},{0,24},{4,28},{40,32},... | collective-permute-start | bytes 2359304 | tf_op jit(solution)/shard_map/ppermute | solution.py:31
  144.0 38.6 %collective-permute-start.18 = (bf16[2,96,2048]{2,1,0:T(8,128)(2,1)}, bf16[2,96,2048]{2,1,0:T(8,128)(2,1)S(1)}, u32[]{:S(2)}, u32[]{:S(2)}) collective-permute-start(bf16[2,96,2048]{2,1,0:T(8,128)(2,1)} %get-tuple-element.61), channel_id=1, source_target_pairs={{16,0},{20,4},{24,8},{28,12},{0,16},{4,20},{8,24},{12,28},{48,32},... | collective-permute-start | bytes 2359304 | tf_op jit(solution)/shard_map/ppermute | solution.py:31
  144.0 39.1 %collective-permute-start.19 = (bf16[2,96,2048]{2,1,0:T(8,128)(2,1)}, bf16[2,96,2048]{2,1,0:T(8,128)(2,1)S(1)}, u32[]{:S(2)}, u32[]{:S(2)}) collective-permute-start(bf16[2,96,2048]{2,1,0:T(8,128)(2,1)} %get-tuple-element.62), channel_id=1, source_target_pairs={{24,0},{28,4},{0,8},{4,12},{8,16},{12,20},{16,24},{20,28},{56,32},... | collective-permute-start | bytes 2359304 | tf_op jit(solution)/shard_map/ppermute | solution.py:31
  144.7 39.9 %collective-permute-start.32 = (bf16[2,96,2048]{2,1,0:T(8,128)(2,1)}, bf16[2,96,2048]{2,1,0:T(8,128)(2,1)}, u32[]{:S(2)}, u32[]{:S(2)}) collective-permute-start(bf16[2,96,2048]{2,1,0:T(8,128)(2,1)} %get-tuple-element.76), channel_id=1, source_target_pairs={{32,0},{36,4},{40,8},{44,12},{48,16},{52,20},{56,24},{60,28},{64,3... | collective-permute-start | bytes 2359304 | tf_op jit(solution)/shard_map/ppermute | solution.py:31
  162.3 23.1 %collective-permute-start.33 = (bf16[2,96,2048]{2,1,0:T(8,128)(2,1)}, bf16[2,96,2048]{2,1,0:T(8,128)(2,1)}, u32[]{:S(2)}, u32[]{:S(2)}) collective-permute-start(bf16[2,96,2048]{2,1,0:T(8,128)(2,1)} %get-tuple-element.77), channel_id=1, source_target_pairs={{64,0},{68,4},{72,8},{76,12},{80,16},{84,20},{88,24},{92,28},{96,3... | collective-permute-start | bytes 2359304 | tf_op jit(solution)/shard_map/ppermute | solution.py:31
  182.5 40.7 %copy-start.12 = (bf16[2,96,2048]{2,1,0:T(8,128)(2,1)}, bf16[2,96,2048]{2,1,0:T(8,128)(2,1)S(1)}, u32[]{:S(2)}) copy-start(bf16[2,96,2048]{2,1,0:T(8,128)(2,1)S(1)} %collective-permute-done.17.refs_3_) | copy-start | bytes 2359300
  182.5 20.4 %collective-permute-start.34 = (bf16[2,96,2048]{2,1,0:T(8,128)(2,1)}, bf16[2,96,2048]{2,1,0:T(8,128)(2,1)S(1)}, u32[]{:S(2)}, u32[]{:S(2)}) collective-permute-start(bf16[2,96,2048]{2,1,0:T(8,128)(2,1)} %get-tuple-element.78), channel_id=1, source_target_pairs={{96,0},{100,4},{104,8},{108,12},{112,16},{116,20},{120,24},{124,28... | collective-permute-start | bytes 2359304 | tf_op jit(solution)/shard_map/ppermute | solution.py:31
  182.6 41.0 %copy-start.13 = (bf16[2,96,2048]{2,1,0:T(8,128)(2,1)}, bf16[2,96,2048]{2,1,0:T(8,128)(2,1)S(1)}, u32[]{:S(2)}) copy-start(bf16[2,96,2048]{2,1,0:T(8,128)(2,1)S(1)} %collective-permute-done.18.refs_4_) | copy-start | bytes 2359300
  182.6 21.3 %collective-permute-start.28 = (bf16[2,96,2048]{2,1,0:T(8,128)(2,1)}, bf16[2,96,2048]{2,1,0:T(8,128)(2,1)S(1)}, u32[]{:S(2)}, u32[]{:S(2)}) collective-permute-start(bf16[2,96,2048]{2,1,0:T(8,128)(2,1)} %get-tuple-element.71), channel_id=1, source_target_pairs={{4,0},{0,4},{12,8},{8,12},{20,16},{16,20},{28,24},{24,28},{36,32},... | collective-permute-start | bytes 2359304 | tf_op jit(solution)/shard_map/ppermute | solution.py:31
  183.1 41.2 %copy-start.14 = (bf16[2,96,2048]{2,1,0:T(8,128)(2,1)}, bf16[2,96,2048]{2,1,0:T(8,128)(2,1)S(1)}, u32[]{:S(2)}) copy-start(bf16[2,96,2048]{2,1,0:T(8,128)(2,1)S(1)} %collective-permute-done.19.refs_5_) | copy-start | bytes 2359300
  183.1 20.9 %collective-permute-start.29 = (bf16[2,96,2048]{2,1,0:T(8,128)(2,1)}, bf16[2,96,2048]{2,1,0:T(8,128)(2,1)S(1)}, u32[]{:S(2)}, u32[]{:S(2)}) collective-permute-start(bf16[2,96,2048]{2,1,0:T(8,128)(2,1)} %get-tuple-element.72), channel_id=1, source_target_pairs={{12,0},{8,4},{20,8},{16,12},{28,16},{24,20},{4,24},{0,28},{44,32},... | collective-permute-start | bytes 2359304 | tf_op jit(solution)/shard_map/ppermute | solution.py:31
  184.6 37.8 %collective-permute-start.30 = (bf16[2,96,2048]{2,1,0:T(8,128)(2,1)}, bf16[2,96,2048]{2,1,0:T(8,128)(2,1)S(1)}, u32[]{:S(2)}, u32[]{:S(2)}) collective-permute-start(bf16[2,96,2048]{2,1,0:T(8,128)(2,1)} %get-tuple-element.73), channel_id=1, source_target_pairs={{20,0},{16,4},{28,8},{24,12},{4,16},{0,20},{12,24},{8,28},{52,32},... | collective-permute-start | bytes 2359304 | tf_op jit(solution)/shard_map/ppermute | solution.py:31
  185.4 47.4 %collective-permute-start.31 = (bf16[2,96,2048]{2,1,0:T(8,128)(2,1)}, bf16[2,96,2048]{2,1,0:T(8,128)(2,1)}, u32[]{:S(2)}, u32[]{:S(2)}) collective-permute-start(bf16[2,96,2048]{2,1,0:T(8,128)(2,1)} %get-tuple-element.74), channel_id=1, source_target_pairs={{28,0},{24,4},{4,8},{0,12},{12,16},{8,20},{20,24},{16,28},{60,32},... | collective-permute-start | bytes 2359304 | tf_op jit(solution)/shard_map/ppermute | solution.py:31
  202.9 30.0 %collective-permute-start.35 = (bf16[2,96,2048]{2,1,0:T(8,128)(2,1)}, bf16[2,96,2048]{2,1,0:T(8,128)(2,1)}, u32[]{:S(2)}, u32[]{:S(2)}) collective-permute-start(bf16[2,96,2048]{2,1,0:T(8,128)(2,1)} %get-tuple-element.79), channel_id=1, source_target_pairs={{4,0},{0,4},{12,8},{8,12},{20,16},{16,20},{28,24},{24,28},{36,32},... | collective-permute-start | bytes 2359304 | tf_op jit(solution)/shard_map/ppermute | solution.py:31
  204.0 28.9 %collective-permute-start.36 = (bf16[2,96,2048]{2,1,0:T(8,128)(2,1)}, bf16[2,96,2048]{2,1,0:T(8,128)(2,1)}, u32[]{:S(2)}, u32[]{:S(2)}) collective-permute-start(bf16[2,96,2048]{2,1,0:T(8,128)(2,1)} %get-tuple-element.80), channel_id=1, source_target_pairs={{36,0},{32,4},{44,8},{40,12},{52,16},{48,20},{60,24},{56,28},{68,3... | collective-permute-start | bytes 2359304 | tf_op jit(solution)/shard_map/ppermute | solution.py:31
  204.0 36.8 %collective-permute-start.37 = (bf16[2,96,2048]{2,1,0:T(8,128)(2,1)}, bf16[2,96,2048]{2,1,0:T(8,128)(2,1)}, u32[]{:S(2)}, u32[]{:S(2)}) collective-permute-start(bf16[2,96,2048]{2,1,0:T(8,128)(2,1)} %get-tuple-element.81), channel_id=1, source_target_pairs={{68,0},{64,4},{76,8},{72,12},{84,16},{80,20},{92,24},{88,28},{100,... | collective-permute-start | bytes 2359304 | tf_op jit(solution)/shard_map/ppermute | solution.py:31
  223.2 34.3 %collective-permute-start.38 = (bf16[2,96,2048]{2,1,0:T(8,128)(2,1)}, bf16[2,96,2048]{2,1,0:T(8,128)(2,1)}, u32[]{:S(2)}, u32[]{:S(2)}) collective-permute-start(bf16[2,96,2048]{2,1,0:T(8,128)(2,1)} %get-tuple-element.82), channel_id=1, source_target_pairs={{100,0},{96,4},{108,8},{104,12},{116,16},{112,20},{124,24},{120,28... | collective-permute-start | bytes 2359304 | tf_op jit(solution)/shard_map/ppermute | solution.py:31
  265.6 38.1 %copy-start.19 = (bf16[128,2048]{1,0:T(8,128)(2,1)S(1)}, bf16[128,2048]{1,0:T(8,128)(2,1)}, u32[]{:S(2)}) copy-start(bf16[128,2048]{1,0:T(8,128)(2,1)} %get-tuple-element.90) | copy-start | bytes 1572868
  265.6 9.0 %collective-permute-start.39 = (bf16[64,2048]{1,0:T(8,128)(2,1)}, bf16[64,2048]{1,0:T(8,128)(2,1)S(1)}, u32[]{:S(2)}, u32[]{:S(2)}) collective-permute-start(bf16[64,2048]{1,0:T(8,128)(2,1)} %get-tuple-element.85), channel_id=1, source_target_pairs={{96,0},{100,4},{104,8},{108,12},{112,16},{116,20},{120,24},{124,28... | collective-permute-start | bytes 786440 | tf_op jit(solution)/shard_map/ppermute | solution.py:31
  265.7 24.8 %collective-permute-start.41 = (bf16[64,2048]{1,0:T(8,128)(2,1)}, bf16[64,2048]{1,0:T(8,128)(2,1)S(1)}, u32[]{:S(2)}, u32[]{:S(2)}) collective-permute-start(bf16[64,2048]{1,0:T(8,128)(2,1)} %get-tuple-element.86), channel_id=1, source_target_pairs={{32,0},{36,4},{40,8},{44,12},{48,16},{52,20},{56,24},{60,28},{64,3... | collective-permute-start | bytes 786440 | tf_op jit(solution)/shard_map/ppermute | solution.py:31
  268.4 22.3 %collective-permute-start.42 = (bf16[64,2048]{1,0:T(8,128)(2,1)}, bf16[64,2048]{1,0:T(8,128)(2,1)S(1)}, u32[]{:S(2)}, u32[]{:S(2)}) collective-permute-start(bf16[64,2048]{1,0:T(8,128)(2,1)} %get-tuple-element.87), channel_id=1, source_target_pairs={{96,0},{100,4},{104,8},{108,12},{112,16},{116,20},{120,24},{124,28... | collective-permute-start | bytes 786440 | tf_op jit(solution)/shard_map/ppermute | solution.py:31
  268.4 10.9 %collective-permute-start.43 = (bf16[64,2048]{1,0:T(8,128)(2,1)}, bf16[64,2048]{1,0:T(8,128)(2,1)S(1)}, u32[]{:S(2)}, u32[]{:S(2)}) collective-permute-start(bf16[64,2048]{1,0:T(8,128)(2,1)} %get-tuple-element.89), channel_id=1, source_target_pairs={{32,0},{36,4},{40,8},{44,12},{48,16},{52,20},{56,24},{60,28},{64,3... | collective-permute-start | bytes 786440 | tf_op jit(solution)/shard_map/ppermute | solution.py:31
  271.0 11.8 %collective-permute-start.45 = (bf16[64,2048]{1,0:T(8,128)(2,1)}, bf16[64,2048]{1,0:T(8,128)(2,1)S(1)}, u32[]{:S(2)}, u32[]{:S(2)}) collective-permute-start(bf16[64,2048]{1,0:T(8,128)(2,1)} %get-tuple-element.92), channel_id=1, source_target_pairs={{24,0},{28,4},{0,8},{4,12},{8,16},{12,20},{16,24},{20,28},{56,32},... | collective-permute-start | bytes 786440 | tf_op jit(solution)/shard_map/ppermute | solution.py:31
  274.6 21.0 %collective-permute-start.47 = (bf16[64,2048]{1,0:T(8,128)(2,1)}, bf16[64,2048]{1,0:T(8,128)(2,1)S(1)}, u32[]{:S(2)}, u32[]{:S(2)}) collective-permute-start(bf16[64,2048]{1,0:T(8,128)(2,1)} %get-tuple-element.93), channel_id=1, source_target_pairs={{8,0},{12,4},{16,8},{20,12},{24,16},{28,20},{0,24},{4,28},{40,32},... | collective-permute-start | bytes 786440 | tf_op jit(solution)/shard_map/ppermute | solution.py:31
  279.3 8.7 %collective-permute-start.49 = (bf16[64,2048]{1,0:T(8,128)(2,1)}, bf16[64,2048]{1,0:T(8,128)(2,1)S(1)}, u32[]{:S(2)}, u32[]{:S(2)}) collective-permute-start(bf16[64,2048]{1,0:T(8,128)(2,1)} %get-tuple-element.96), channel_id=1, source_target_pairs={{8,0},{12,4},{16,8},{20,12},{24,16},{28,20},{0,24},{4,28},{40,32},... | collective-permute-start | bytes 786440 | tf_op jit(solution)/shard_map/ppermute | solution.py:31
  282.9 9.5 %collective-permute-start.40 = (bf16[64,2048]{1,0:T(8,128)(2,1)S(1)}, bf16[64,2048]{1,0:T(8,128)(2,1)S(1)}, u32[]{:S(2)}, u32[]{:S(2)}) collective-permute-start(bf16[64,2048]{1,0:T(8,128)(2,1)S(1)} %add_convert_fusion.8), channel_id=1, source_target_pairs={{96,0},{100,4},{104,8},{108,12},{112,16},{116,20},{120,24},{124,28... | collective-permute-start | bytes 786440 | tf_op jit(solution)/shard_map/ppermute | solution.py:31
  288.0 6.3 %collective-permute-start.44 = (bf16[64,2048]{1,0:T(8,128)(2,1)S(1)}, bf16[64,2048]{1,0:T(8,128)(2,1)S(1)}, u32[]{:S(2)}, u32[]{:S(2)}) collective-permute-start(bf16[64,2048]{1,0:T(8,128)(2,1)S(1)} %add_convert_fusion.6), channel_id=1, source_target_pairs={{32,0},{36,4},{40,8},{44,12},{48,16},{52,20},{56,24},{60,28},{64,3... | collective-permute-start | bytes 786440 | tf_op jit(solution)/shard_map/ppermute | solution.py:31
  290.5 7.3 %collective-permute-start.48 = (bf16[64,2048]{1,0:T(8,128)(2,1)}, bf16[64,2048]{1,0:T(8,128)(2,1)S(1)}, u32[]{:S(2)}, u32[]{:S(2)}) collective-permute-start(bf16[64,2048]{1,0:T(8,128)(2,1)} %get-tuple-element.94), channel_id=1, source_target_pairs={{24,0},{28,4},{0,8},{4,12},{8,16},{12,20},{16,24},{20,28},{56,32},... | collective-permute-start | bytes 786440 | tf_op jit(solution)/shard_map/ppermute | solution.py:31
  290.6 13.0 %collective-permute-start.46 = (bf16[64,2048]{1,0:T(8,128)(2,1)S(1)}, bf16[64,2048]{1,0:T(8,128)(2,1)S(1)}, u32[]{:S(2)}, u32[]{:S(2)}) collective-permute-start(bf16[64,2048]{1,0:T(8,128)(2,1)S(1)} %add_convert_fusion.4), channel_id=1, source_target_pairs={{24,0},{28,4},{0,8},{4,12},{8,16},{12,20},{16,24},{20,28},{56,32},... | collective-permute-start | bytes 786440 | tf_op jit(solution)/shard_map/ppermute | solution.py:31
  292.4 11.3 %collective-permute-start.50 = (bf16[64,2048]{1,0:T(8,128)(2,1)S(1)}, bf16[64,2048]{1,0:T(8,128)(2,1)S(1)}, u32[]{:S(2)}, u32[]{:S(2)}) collective-permute-start(bf16[64,2048]{1,0:T(8,128)(2,1)S(1)} %add_convert_fusion.2), channel_id=1, source_target_pairs={{8,0},{12,4},{16,8},{20,12},{24,16},{28,20},{0,24},{4,28},{40,32},... | collective-permute-start | bytes 786440 | tf_op jit(solution)/shard_map/ppermute | solution.py:31
  304.0 6.9 %collective-permute-start.52 = (bf16[128,1024]{1,0:T(8,128)(2,1)S(1)}, bf16[128,1024]{1,0:T(8,128)(2,1)S(1)}, u32[]{:S(2)}, u32[]{:S(2)}) collective-permute-start(bf16[128,1024]{1,0:T(8,128)(2,1)S(1)} %pad_maximum_fusion.2), channel_id=1, source_target_pairs={{2,0},{3,1},{0,2},{1,3},{6,4},{7,5},{4,6},{5,7},{10,8},{11,9},{8,1... | collective-permute-start | bytes 786440 | tf_op jit(solution)/shard_map/ppermute | solution.py:27
  304.5 13.9 %collective-permute-start.51 = (bf16[128,1024]{1,0:T(8,128)(2,1)S(1)}, bf16[128,1024]{1,0:T(8,128)(2,1)S(1)}, u32[]{:S(2)}, u32[]{:S(2)}) collective-permute-start(bf16[128,1024]{1,0:T(8,128)(2,1)S(1)} %pad_maximum_fusion.1), channel_id=1, source_target_pairs={{3,0},{0,1},{1,2},{2,3},{7,4},{4,5},{5,6},{6,7},{11,8},{8,9},{9,10... | collective-permute-start | bytes 786440 | tf_op jit(solution)/shard_map/ppermute | solution.py:27
  304.6 13.8 %collective-permute-start.53 = (bf16[128,1024]{1,0:T(8,128)(2,1)S(1)}, bf16[128,1024]{1,0:T(8,128)(2,1)S(1)}, u32[]{:S(2)}, u32[]{:S(2)}) collective-permute-start(bf16[128,1024]{1,0:T(8,128)(2,1)S(1)} %fusion.7), channel_id=1, source_target_pairs={{1,0},{2,1},{3,2},{0,3},{5,4},{6,5},{7,6},{4,7},{9,8},{10,9},{11,1... | collective-permute-start | bytes 786440 | tf_op jit(solution)/shard_map/ppermute | solution.py:27
  (10 other events, 102.4 us)
